TPU v7x, 32 devices: a whole 2x2x4 slice. The times are simulated.
32 devices in a mesh: rows: 8 (over z, y), chan: 4 (over x, core).
Axes of the slice: x: 2, y: 2, z: 4, core: 2. Of those that a mesh axis runs over, the one named last changes fastest.
Arguments:
- radiances: float32 [16, 16384], P('chan', 'rows'), may hold values from -6 to 6
- band: int32 [16384, 1], P('rows'), may hold values from 0 to 7; in each aligned block of 2048 rows (0 to 2047, 2048 to 4095, ...) at most 512 rows name the same one
- row_in_band: int32 [16384], P('rows'), may hold values from 0 to 3
- column: int32 [16384], P('rows'), may hold values from 0 to 1439
Outputs:
- cell_count: int32 [32, 1440], P('rows')
- cell_mean: float32 [16, 32, 1440], P('chan', 'rows')
- cell_var: float32 [16, 32, 1440], P('chan', 'rows')
- cell_spread: float32 [32, 1440], P('rows')
- departure: float32 [16, 16384], P('chan', 'rows')
Inputs may be any that keep to these rules, and one draw needn't show every extreme that they name: Within each aligned block of 2048 observations (one scan-time shard) no band is named by more than 512 observations, and in some blocks one band is named by exactly 512.
All inputs are finite; a program needn't handle non-finite values.
Results may differ from a plain program's by a relative error of at most 0.0003.
Values sent between devices are 32-bit elements.
A program may use at most 64 MiB of HBM per device.

v0:
```python
import functools

import jax
import jax.numpy as jnp
from jax import lax
from jax.experimental import pallas as pl
from jax.experimental.pallas import tpu as pltpu
from jax.sharding import PartitionSpec as P

CHAN = 16
COLS = 1440
ROWS_DEV = 4
LOW = 256
LANES = 128
BLOCKS = -(-COLS // LOW)
QS = BLOCKS * ROWS_DEV
F32 = jnp.float32
BF16 = jnp.bfloat16
MESH = pl.DeviceIdType.MESH
NT = (((1,), (1,)), ((), ()))
NN = (((1,), (0,)), ((), ()))


def iota(shape, axis):
    return lax.broadcasted_iota(jnp.int32, shape, axis)


def onehot(mask):
    return jnp.where(mask, 1.0, 0.0)


def two(values):
    high = values.astype(BF16).astype(F32)
    return high, values - high


def dot(a, b, dims):
    return lax.dot_general(a, b, dims, preferred_element_type=F32)


def rank_of(dest, nrows):
    obs = dest.shape[1]
    nblock = obs // 128
    hot = onehot(iota((nrows, obs), 0) == dest)
    stacked = jnp.concatenate([hot[:, b * 128 : (b + 1) * 128] for b in range(nblock)], axis=0)
    stacked_b = stacked.astype(BF16)
    size = nblock * nrows
    upper = onehot(iota((128, 128), 0) <= iota((128, 128), 1)).astype(BF16)
    inner = dot(stacked_b, upper, NN)
    r, c = iota((size, size), 0), iota((size, size), 1)
    earlier = onehot((c < r) & (lax.rem(r - c + size, nrows) == 0)).astype(BF16)
    before = jnp.sum(dot(earlier, stacked_b, NN), axis=1, keepdims=True)
    ranks = stacked * (inner + before)
    rows = [
        jnp.sum(ranks[b * nrows : (b + 1) * nrows], axis=0, keepdims=True) for b in range(nblock)
    ]
    return (jnp.concatenate(rows, axis=1) - 1.0).astype(jnp.int32)


def spill(out, values):
    for j in range(BLOCKS):
        start = j * LOW
        width = min(LOW, COLS - start)
        out[:, start : start + width] = values[j * ROWS_DEV : (j + 1) * ROWS_DEV, :width].astype(
            out.dtype
        )


def kernel(
    nrows,
    nchan,
    rad_in,
    band_in,
    rib_in,
    col_in,
    cnt_out,
    mean_out,
    var_out,
    spr_out,
    diff_out,
    scale_out,
    rank_out,
    dest_out,
    rank_hot,
    rad_ref,
    band_ref,
    rib_ref,
    col_ref,
    col_hot,
    q_hot,
    acc,
    send_v,
    send_c,
    recv_v,
    recv_c,
    parts,
    back_s,
    back_r,
    scale_s,
    scale_r,
    ins,
    sv,
    rv,
    sc,
    rc,
    sp,
    rp,
    sb,
    rb,
    ss,
    rs,
):
    me = lax.axis_index("rows")
    mc = lax.axis_index("chan")
    fields, obs = rad_ref.shape
    cap = rank_hot.shape[0]

    fetches = [
        pltpu.make_async_copy(a, b, ins.at[i])
        for i, (a, b) in enumerate(
            ((band_in, band_ref), (rad_in, rad_ref), (rib_in, rib_ref), (col_in, col_ref))
        )
    ]
    for fetch in fetches:
        fetch.start()
    barrier = pltpu.get_barrier_semaphore()
    for d in range(nrows):
        for e in range(nchan):
            if d + e > 0:
                to = {"rows": lax.rem(me + d, nrows), "chan": lax.rem(mc + e, nchan)}
                pl.semaphore_signal(barrier, inc=1, device_id=to, device_id_type=MESH)

    fetches[0].wait()
    dest = band_ref[...]
    dest_out[...] = dest
    rank = rank_of(dest, nrows)
    rank_out[...] = rank
    rank_hot[...] = onehot(iota((cap, obs), 0) == rank).astype(BF16)
    for fetch in fetches[1:]:
        fetch.wait()
    rad = rad_ref[...]
    high, rest = two(rad)
    middle, low = two(rest)
    col = col_ref[...]
    code = (col // LOW) * ROWS_DEV + rib_ref[...] + 1
    pad = -(3 * fields + 2) % 8
    group = 3 * fields + 2 + pad
    payload = jnp.concatenate(
        [high, middle, low, code.astype(F32), (col % LOW).astype(F32), jnp.zeros((pad, obs), F32)],
        axis=0,
    )
    left = jnp.concatenate(
        [jnp.where(dest == lax.rem(me + d, nrows), payload, 0.0) for d in range(nrows)], axis=0
    ).astype(BF16)
    placed = dot(left, rank_hot[...], NT)
    pl.semaphore_wait(barrier, nrows * nchan - 1)

    out_copies = []
    for d in list(range(1, nrows)) + [0]:
        part = placed[d * group : (d + 1) * group]
        values = (part[:fields] + part[fields : 2 * fields]) + part[2 * fields : 3 * fields]
        cells = part[3 * fields : 3 * fields + 1] * LOW + part[3 * fields + 1 : 3 * fields + 2]
        if d == 0:
            recv_v[0] = values
            recv_c[0] = cells
            continue
        send_v[d] = values
        send_c[d] = cells
        to = {"rows": lax.rem(me + d, nrows)}
        for src, dst, s, r in ((send_v, recv_v, sv, rv), (send_c, recv_c, sc, rc)):
            copy = pltpu.make_async_remote_copy(
                src_ref=src.at[d],
                dst_ref=dst.at[d],
                send_sem=s.at[d],
                recv_sem=r.at[d],
                device_id=to,
                device_id_type=MESH,
            )
            copy.start()
            out_copies.append(copy)

    for d in range(nrows):
        if d > 0:
            out_copies[2 * d - 2].wait_recv()
            out_copies[2 * d - 1].wait_recv()
        values = recv_v[d]
        cells = recv_c[d].astype(jnp.int32)
        cols_t = onehot(iota((LOW, cap), 0) == (cells & (LOW - 1))).astype(BF16)
        col_hot[d] = cols_t
        quads = onehot(iota((QS, cap), 0) == (cells // LOW) - 1)
        q_hot[d] = quads
        features = two(values) + two(values * values)
        rows = [quads] + [quads * x[f : f + 1] for x in features for f in range(fields)]
        sums = dot(jnp.concatenate(rows, axis=0).astype(BF16), cols_t, NT)
        if d == 0:
            acc[...] = sums
        else:
            acc[...] += sums

    count = acc[0:QS]
    inverse = 1.0 / jnp.maximum(count, 1.0)
    means, variances = [], []
    for f in range(fields):

        def total(k):
            at = (1 + k * fields + f) * QS
            after = at + fields * QS
            return acc[at : at + QS] + acc[after : after + QS]

        mean = total(0) * inverse
        means.append(mean)
        variances.append(jnp.maximum(total(2) * inverse - mean * mean, 0.0))
    partial = variances[0]
    for f in range(1, fields):
        partial = partial + variances[f]
    split = [two(mean) for mean in means]
    split.append(two(partial))
    table = jnp.concatenate([x[0] for x in split] + [x[1] for x in split], axis=0).astype(BF16)
    back_copies = []
    scale_copies = []
    for d in list(range(nrows - 1, 0, -1)) + [0]:
        picked = dot(table, col_hot[d], NN)
        quads = q_hot[d]
        found = []
        for f in range(fields + 1):
            at = (fields + 1 + f) * QS
            both = picked[f * QS : (f + 1) * QS] + picked[at : at + QS]
            found.append(jnp.sum(both * quads, axis=0, keepdims=True))
        diff = recv_v[d] - jnp.concatenate(found[:fields], axis=0)
        scale_s[d] = found[fields]
        if d == 0:
            back_r[0] = diff
            scale_r[0] = found[fields]
        if d > 0:
            back_s[d] = diff
            copy = pltpu.make_async_remote_copy(
                src_ref=back_s.at[d],
                dst_ref=back_r.at[d],
                send_sem=sb.at[d],
                recv_sem=rb.at[d],
                device_id={"rows": lax.rem(me + nrows - d, nrows)},
                device_id_type=MESH,
            )
            copy.start()
            back_copies.append(copy)
        for e in range(nchan):
            if d + e == 0:
                continue
            slot = e * nrows + d
            copy = pltpu.make_async_remote_copy(
                src_ref=scale_s.at[d],
                dst_ref=scale_r.at[slot],
                send_sem=ss.at[slot],
                recv_sem=rs.at[slot],
                device_id={
                    "rows": lax.rem(me + nrows - d, nrows),
                    "chan": lax.rem(mc + e, nchan),
                },
                device_id_type=MESH,
            )
            copy.start()
            scale_copies.append(copy)

    parts[mc] = partial
    part_copies = []
    for d in range(1, nchan):
        copy = pltpu.make_async_remote_copy(
            src_ref=parts.at[mc],
            dst_ref=parts.at[mc],
            send_sem=sp.at[d],
            recv_sem=rp.at[d],
            device_id={"chan": lax.rem(mc + d, nchan)},
            device_id_type=MESH,
        )
        copy.start()
        part_copies.append(copy)

    spill(cnt_out, count)
    for f in range(fields):
        spill(mean_out.at[f], means[f])
        spill(var_out.at[f], variances[f])

    for copy in back_copies:
        copy.wait_recv()
    diff_out[...] = back_r[...]
    for copy in part_copies:
        copy.wait_recv()
    spread = parts[0]
    for c in range(1, nchan):
        spread = spread + parts[c]
    spill(spr_out, spread)
    for copy in scale_copies:
        copy.wait_recv()
    spreads = None
    for e in range(nchan):
        rows = jnp.concatenate([scale_r[e * nrows + d] for d in range(nrows)], axis=0)
        spreads = rows if spreads is None else spreads + rows
    scale_out[...] = lax.rsqrt(1.0 + spreads / CHAN)

    for copy in out_copies + part_copies + back_copies + scale_copies:
        copy.wait_send()


def finish(
    nrows,
    cnt_ref,
    mean_ref,
    var_ref,
    spr_ref,
    diff_ref,
    scale_ref,
    rank_ref,
    dest_ref,
    cnt_out,
    mean_out,
    var_out,
    spr_out,
    dep_out,
    sems,
):
    pairs = ((mean_ref, mean_out), (var_ref, var_out), (cnt_ref, cnt_out), (spr_ref, spr_out))
    copies = [pltpu.make_async_copy(a, b, sems.at[i]) for i, (a, b) in enumerate(pairs)]
    for copy in copies:
        copy.start()
    me = lax.axis_index("rows")
    fields, obs = dep_out.shape
    tiles = -(-scale_ref.shape[1] // LANES)
    lines = obs // LANES

    def folded(ref):
        return jnp.concatenate(
            [ref[:, k * LANES : (k + 1) * LANES] for k in range(lines)], axis=0
        )

    rank = folded(rank_ref)
    distance = lax.rem(folded(dest_ref) - me + nrows, nrows)
    place = distance * tiles + rank // LANES
    lane = rank & (LANES - 1)
    found = [jnp.zeros((lines, LANES), F32) for _ in range(fields + 1)]
    for d in range(nrows):
        for t in range(tiles):
            here = place == d * tiles + t
            span = slice(t * LANES, (t + 1) * LANES)
            for f in range(fields + 1):
                row = scale_ref[d : d + 1, span] if f == fields else diff_ref[d, f : f + 1, span]
                taken = jnp.take_along_axis(
                    jnp.broadcast_to(row, (lines, LANES)), lane, axis=1, mode="promise_in_bounds"
                )
                found[f] = jnp.where(here, taken, found[f])
    results = [found[f] * found[fields] for f in range(fields)]
    for k in range(lines):
        dep_out[:, k * LANES : (k + 1) * LANES] = jnp.concatenate(
            [x[k : k + 1] for x in results], axis=0
        )
    for copy in copies:
        copy.wait()


def body(radiances, band, row_in_band, column):
    nrows = lax.axis_size("rows")
    nchan = lax.axis_size("chan")
    fields, obs = radiances.shape
    cap = 2 * obs // nrows
    nfeat = 1 + 4 * fields
    vmem = pl.BlockSpec(memory_space=pltpu.VMEM)
    anywhere = pl.BlockSpec(memory_space=pl.ANY)
    dma = pltpu.SemaphoreType.DMA
    band = band.reshape(1, obs)
    shapes = (
        ((ROWS_DEV, COLS), jnp.int32),
        ((fields, ROWS_DEV, COLS), F32),
        ((fields, ROWS_DEV, COLS), F32),
        ((ROWS_DEV, COLS), F32),
    )
    held = pl.pallas_call(
        functools.partial(kernel, nrows, nchan),
        out_shape=tuple(pltpu.VMEM(s, t) for s, t in shapes)
        + (
            pltpu.VMEM((nrows, fields, cap), F32),
            pltpu.VMEM((nrows, cap), F32),
            pltpu.VMEM((1, obs), jnp.int32),
            pltpu.VMEM((1, obs), jnp.int32),
        ),
        in_specs=[pl.BlockSpec(memory_space=pltpu.HBM)] * 4,
        out_specs=(vmem,) * 8,
        scratch_shapes=[
            pltpu.VMEM((cap, obs), BF16),
            pltpu.VMEM((fields, obs), F32),
            pltpu.VMEM((1, obs), jnp.int32),
            pltpu.VMEM((1, obs), jnp.int32),
            pltpu.VMEM((1, obs), jnp.int32),
            pltpu.VMEM((nrows, LOW, cap), BF16),
            pltpu.VMEM((nrows, QS, cap), F32),
            pltpu.VMEM((nfeat * QS, LOW), F32),
            pltpu.VMEM((nrows, fields, cap), F32),
            pltpu.VMEM((nrows, 1, cap), F32),
            pltpu.VMEM((nrows, fields, cap), F32),
            pltpu.VMEM((nrows, 1, cap), F32),
            pltpu.VMEM((nchan, QS, LOW), F32),
            pltpu.VMEM((nrows, fields, cap), F32),
            pltpu.VMEM((nrows, fields, cap), F32),
            pltpu.VMEM((nrows, 1, cap), F32),
            pltpu.VMEM((nchan * nrows, 1, cap), F32),
            dma((4,)),
            dma((nrows,)),
            dma((nrows,)),
            dma((nrows,)),
            dma((nrows,)),
            dma((nchan,)),
            dma((nchan,)),
            dma((nrows,)),
            dma((nrows,)),
            dma((nchan * nrows,)),
            dma((nchan * nrows,)),
        ],
        compiler_params=pltpu.CompilerParams(
            collective_id=0, has_side_effects=True, vmem_limit_bytes=32 * 1024 * 1024
        ),
    )(
        *(
            pltpu.with_memory_space_constraint(x, pltpu.HBM)
            for x in (radiances, band, row_in_band.reshape(1, obs), column.reshape(1, obs))
        )
    )
    return pl.pallas_call(
        functools.partial(finish, nrows),
        out_shape=tuple(jax.ShapeDtypeStruct(s, t) for s, t in shapes)
        + (jax.ShapeDtypeStruct((fields, obs), F32),),
        in_specs=[vmem] * 8,
        out_specs=(anywhere,) * 4 + (vmem,),
        scratch_shapes=[dma((4,))],
        compiler_params=pltpu.CompilerParams(vmem_limit_bytes=32 * 1024 * 1024),
    )(*held)


def solution(mesh):
    in_specs = (P("chan", "rows"), P("rows", None), P("rows"), P("rows"))
    out_specs = (
        P("rows", None),
        P("chan", "rows", None),
        P("chan", "rows", None),
        P("rows", None),
        P("chan", "rows"),
    )
    return jax.shard_map(body, mesh=mesh, in_specs=in_specs, out_specs=out_specs, check_vma=False)
```

profile of v0, /device:TPU:0, one launch (start us, length us, event | category | flops | bytes accessed | tf_op | source)
XLA Modules:
  0.0 20.2 jit_solution(4486010916635207075)
XLA Ops:
  0.6 18.1 %shard_map.83 = (s32[4,1440]{1,0:T(4,128)S(1)}, f32[4,4,1440]{2,1,0:T(4,128)S(1)}, f32[4,4,1440]{2,1,0:T(4,128)S(1)}, f32[4,1440]{1,0:T(4,128)S(1)}, f32[8,4,512...) custom-call(f32[4,2048]{1,0:T(4,128)} %rad_in.1, s32[1,2048]{1,0:T(1,128)} %bitcast.3, ...), custom_call_target="tpu_custom_call" | custom-call | tf_op jit(solution)/shard_map/pallas_call | solution.py:375
  18.8 1.4 %shard_map.84 = (s32[4,1440]{1,0:T(4,128)}, f32[4,4,1440]{2,1,0:T(4,128)}, f32[4,4,1440]{2,1,0:T(4,128)}, f32[4,1440]{1,0:T(4,128)}, f32[4,2048]{1,0:T(4,128)}) custom-call(s32[4,1440]{1,0:T(4,128)S(1)} %get-tuple-element.13.cnt_ref, f32[4,4,1440]{2,1,0:T(4,128)S(1)} %get-tuple-element.14.mean_ref, f32[4,4,1440]{2,1,0:T(4,128)S(1)} %get-tuple-element.15.var_ref, ...), custom_call_target="tpu_custom_call" | custom-call | tf_op jit(solution)/shard_map/pallas_call | solution.py:425
where the time goes:
time: 20.4 us; the launch traced here: 20.2 us
  Pallas kernels  19.5 us (96%)
  between operations  0.64 us (3%)
    pallas_call x1, Pallas kernels, body(): pl.pallas_call(functools.partial(kernel, nrows, nchan), out_shape=tuple((...  18.1 us
    pallas_call x1, Pallas kernels, body(): pl.pallas_call(functools.partial(finish, nrows), out_shape=tuple((jax.Sha...  1.38 us

commit v1 on v0

v1 whole, which is shorter than its diff:
```python
import functools

import jax
import jax.numpy as jnp
from jax import lax
from jax.experimental import pallas as pl
from jax.experimental.pallas import tpu as pltpu
from jax.sharding import PartitionSpec as P

CHAN = 16
COLS = 1440
ROWS_DEV = 4
LOW = 256
LANES = 128
BLOCKS = -(-COLS // LOW)
QS = BLOCKS * ROWS_DEV
F32 = jnp.float32
BF16 = jnp.bfloat16
MESH = pl.DeviceIdType.MESH
NT = (((1,), (1,)), ((), ()))
NN = (((1,), (0,)), ((), ()))


def iota(shape, axis):
    return lax.broadcasted_iota(jnp.int32, shape, axis)


def onehot(mask):
    return jnp.where(mask, 1.0, 0.0)


def two(values):
    high = values.astype(BF16).astype(F32)
    return high, values - high


def dot(a, b, dims):
    return lax.dot_general(a, b, dims, preferred_element_type=F32)


def flip(index, bits):
    out, bit = index, 1
    while bit <= bits:
        if bits & bit:
            out = out + bit - 2 * bit * ((index // bit) % 2)
        bit *= 2
    return out


def rank_of(dest, nrows):
    obs = dest.shape[1]
    nblock = obs // 128
    hot = onehot(iota((nrows, obs), 0) == dest)
    stacked = jnp.concatenate([hot[:, b * 128 : (b + 1) * 128] for b in range(nblock)], axis=0)
    stacked_b = stacked.astype(BF16)
    size = nblock * nrows
    upper = onehot(iota((128, 128), 0) <= iota((128, 128), 1)).astype(BF16)
    inner = dot(stacked_b, upper, NN)
    r, c = iota((size, size), 0), iota((size, size), 1)
    earlier = onehot((c < r) & (lax.rem(r - c + size, nrows) == 0)).astype(BF16)
    before = jnp.sum(dot(earlier, stacked_b, NN), axis=1, keepdims=True)
    ranks = stacked * (inner + before)
    rows = [
        jnp.sum(ranks[b * nrows : (b + 1) * nrows], axis=0, keepdims=True) for b in range(nblock)
    ]
    return (jnp.concatenate(rows, axis=1) - 1.0).astype(jnp.int32)


def spill(out, values):
    for j in range(BLOCKS):
        start = j * LOW
        width = min(LOW, COLS - start)
        out[:, start : start + width] = values[j * ROWS_DEV : (j + 1) * ROWS_DEV, :width].astype(
            out.dtype
        )


def folded(row):
    lines = row.shape[1] // LANES
    return jnp.concatenate([row[:, k * LANES : (k + 1) * LANES] for k in range(lines)], axis=0)


def take(row, lane):
    return jnp.take_along_axis(
        jnp.broadcast_to(row, lane.shape), lane, axis=1, mode="promise_in_bounds"
    )


def look(grids, cells):
    tile, lane = cells // LANES - LOW // LANES, cells & (LANES - 1)
    found = [jnp.zeros(cells.shape, F32) for _ in grids]
    for q in range(QS):
        for half in range(LOW // LANES):
            here = tile == q * (LOW // LANES) + half
            span = slice(half * LANES, (half + 1) * LANES)
            for g, grid in enumerate(grids):
                found[g] = jnp.where(here, take(grid[q : q + 1, span], lane), found[g])
    return found


def sums_of(arrived, slots):
    fields, lines = arrived.shape[1] - 1, arrived.shape[2]
    left, right = [], []
    for d in slots:
        cells = arrived[d, fields].astype(jnp.int32)
        low, high = cells & (LOW - 1), cells // LOW - 1
        features = []
        for f in range(fields):
            x = arrived[d, f]
            features.append(two(x) + two(x * x))
        for t in range(lines):
            right.append(onehot(iota((LOW, LANES), 0) == low[t : t + 1]).astype(BF16))
            quads = onehot(iota((QS, LANES), 0) == high[t : t + 1])
            rows = [quads]
            for k in range(4):
                rows += [quads * features[f][k][t : t + 1] for f in range(fields)]
            left.append(jnp.concatenate(rows, axis=0).astype(BF16))
    return dot(jnp.concatenate(left, axis=1), jnp.concatenate(right, axis=1), NT)


def kernel(
    nrows,
    nchan,
    rad_in,
    band_in,
    rib_in,
    col_in,
    cnt_out,
    mean_out,
    var_out,
    spr_out,
    dep_out,
    rad_ref,
    band_ref,
    rib_ref,
    col_ref,
    rank_hot,
    staged,
    sent,
    arrived,
    grid,
    part_s,
    part_r,
    pair,
    pairs,
    back_s,
    back_r,
    scale_s,
    scale_r,
    turned,
    ready,
    ins,
    so,
    ro,
    sp,
    rp,
    sg,
    rg,
    sb,
    rb,
    ss,
    rs,
):
    me = lax.axis_index("rows")
    mc = lax.axis_index("chan")
    fields, obs = rad_ref.shape
    cap = rank_hot.shape[0]
    lines = cap // LANES
    npair = nchan // 2
    far = list(range(nrows - 1, 0, -1))
    row_peer = [flip(me, d) for d in range(nrows)]
    chan_peer = [lax.rem(mc + 2 * j, nchan) for j in range(npair)]
    partner = flip(mc, 1)

    def remote(src, dst, send, recv, **to):
        return pltpu.make_async_remote_copy(
            src_ref=src,
            dst_ref=dst,
            send_sem=send,
            recv_sem=recv,
            device_id=to,
            device_id_type=MESH,
        )

    barrier = pltpu.get_barrier_semaphore()
    for d in far:
        pl.semaphore_signal(
            barrier, inc=1, device_id={"rows": row_peer[d]}, device_id_type=MESH
        )
    for peer in chan_peer[1:] + [partner]:
        pl.semaphore_signal(barrier, inc=1, device_id={"chan": peer}, device_id_type=MESH)
    fetches = [
        pltpu.make_async_copy(a, b, ins.at[i])
        for i, (a, b) in enumerate(
            ((band_in, band_ref), (rad_in, rad_ref), (rib_in, rib_ref), (col_in, col_ref))
        )
    ]
    for fetch in fetches:
        fetch.start()

    fetches[0].wait()
    dest = band_ref[...]
    rank = rank_of(dest, nrows)
    rank_hot[...] = onehot(iota((cap, obs), 0) == rank).astype(BF16)
    for fetch in fetches[1:]:
        fetch.wait()
    high, rest = two(rad_ref[...])
    middle, low = two(rest)
    col = col_ref[...]
    code = (col // LOW) * ROWS_DEV + rib_ref[...] + 1
    tail = jnp.zeros((8 - fields - 1, obs), F32)
    none = jnp.zeros((1, obs), F32)
    group = 24
    payload = jnp.concatenate(
        [high, (code * LOW).astype(F32), tail]
        + [middle, (col & (LOW - 1)).astype(F32), tail]
        + [low, none, tail],
        axis=0,
    )
    left = jnp.concatenate(
        [jnp.where(dest == row_peer[d], payload, 0.0) for d in range(nrows)], axis=0
    ).astype(BF16)
    placed = dot(left, rank_hot[...], NT)
    for d in range(nrows):
        part = placed[d * group : (d + 1) * group]
        values = (part[0:8] + part[8:16]) + part[16:24]
        for t in range(lines):
            at = (d * lines + t) * 8
            staged[at : at + 8] = values[:, t * LANES : (t + 1) * LANES]
    for d in far + [0]:
        target = sent if d > 0 else arrived
        for f in range(fields + 1):
            target[d, f] = staged[pl.ds(d * lines * 8 + f, lines, stride=8), :]

    pl.semaphore_wait(barrier, nrows - 1 + npair)
    out_copies = {}
    for d in far:
        out_copies[d] = remote(
            sent.at[d], arrived.at[d], so.at[d], ro.at[d], rows=row_peer[d]
        )
        out_copies[d].start()
    for j in range(1, npair):
        pl.semaphore_signal(ready, inc=1, device_id={"chan": chan_peer[j]}, device_id_type=MESH)

    half = nrows // 2
    groups = [[0], list(range(1, half)), list(range(half, nrows))]
    total = None
    for slots in groups:
        for d in slots:
            if d > 0:
                out_copies[d].wait_recv()
        sums = sums_of(arrived, slots)
        total = sums if total is None else total + sums

    def feature(k, f):
        at = (1 + k * fields + f) * QS
        return total[at : at + QS]

    count = total[0:QS]
    inverse = 1.0 / jnp.maximum(count, 1.0)
    partial = None
    means, variances = [], []
    for f in range(fields):
        mean = (feature(0, f) + feature(1, f)) * inverse
        second = (feature(2, f) + feature(3, f)) * inverse
        variance = jnp.maximum(second - mean * mean, 0.0)
        means.append(mean)
        variances.append(variance)
        partial = variance if partial is None else partial + variance
    part_s[...] = partial
    part_copy = remote(part_s, part_r, sp.at[0], rp.at[0], chan=partner)
    part_copy.start()
    for f in range(fields):
        grid[f] = means[f]

    order = far + [0]
    per = max(1, 8 // lines)
    bundles = [order[i : i + per] for i in range(0, nrows, per)]
    cells_of = []
    back_copies = {}
    for slots in bundles:

        def stack(f):
            return jnp.concatenate([arrived[d, f] for d in slots], axis=0)

        cells = stack(fields).astype(jnp.int32)
        cells_of.append(cells)
        found = look([grid.at[f] for f in range(fields)], cells)
        for f in range(fields):
            diff = stack(f) - found[f]
            for i, d in enumerate(slots):
                target = back_s if d > 0 else back_r
                target[d, f] = diff[i * lines : (i + 1) * lines]
        for d in slots:
            if d > 0:
                back_copies[d] = remote(
                    back_s.at[d], back_r.at[d], sb.at[d], rb.at[d], rows=row_peer[d]
                )
                back_copies[d].start()

    part_copy.wait_recv()
    both = part_s[...] + part_r[...]
    pair[...] = both
    mine = mc // 2
    pairs[mine] = both
    pl.semaphore_wait(ready, npair - 1)
    scale_copies = []
    for slots, cells in zip(bundles, cells_of):
        found = look([pair], cells)[0]
        for i, d in enumerate(slots):
            scale_s[d] = found[i * lines : (i + 1) * lines]
            if d == 0:
                scale_r[0] = found[i * lines : (i + 1) * lines]
        for d in slots:
            for j in list(range(1, npair)) + [0]:
                if d + j == 0:
                    continue
                slot = j * nrows + d
                copy = remote(
                    scale_s.at[d],
                    scale_r.at[slot],
                    ss.at[slot],
                    rs.at[slot],
                    rows=row_peer[d],
                    chan=chan_peer[j],
                )
                copy.start()
                scale_copies.append((d, copy))
    pair_copies = []
    for j in range(1, npair):
        copy = remote(pairs.at[mine], pairs.at[mine], sg.at[j], rg.at[j], chan=chan_peer[j])
        copy.start()
        pair_copies.append(copy)

    spill(cnt_out, count)
    for f in range(fields):
        spill(mean_out.at[f], means[f])
        spill(var_out.at[f], variances[f])

    rank = folded(rank)
    place = jnp.bitwise_xor(folded(dest), me) * lines + rank // LANES
    lane = rank & (LANES - 1)
    found = [jnp.zeros(rank.shape, F32) for _ in range(fields + 1)]
    back_order = [0] + list(range(1, half)) + list(range(nrows - 1, half - 1, -1))
    for d in back_order:
        if d > 0:
            back_copies[d].wait_recv()
        for t in range(lines):
            here = place == d * lines + t
            for f in range(fields):
                found[f] = jnp.where(here, take(back_r[d, f, t : t + 1], lane), found[f])
    for copy in pair_copies:
        copy.wait_recv()
    spread = pairs[0]
    for p in range(1, npair):
        spread = spread + pairs[p]
    spill(spr_out, spread)
    for d in back_order:
        for to, copy in scale_copies:
            if to == d:
                copy.wait_recv()
        for t in range(lines):
            here = place == d * lines + t
            row = scale_r[d, t : t + 1]
            for j in range(1, npair):
                row = row + scale_r[j * nrows + d, t : t + 1]
            found[fields] = jnp.where(here, take(row, lane), found[fields])
    scale = lax.rsqrt(1.0 + found[fields] / CHAN)
    many = obs // LANES
    for f in range(fields):
        turned[f * many : (f + 1) * many] = found[f] * scale
    for k in range(many):
        dep_out[:, k * LANES : (k + 1) * LANES] = turned[pl.ds(k, fields, stride=many), :]

    for copy in list(out_copies.values()) + list(back_copies.values()):
        copy.wait_send()
    for copy in [part_copy] + pair_copies + [copy for _, copy in scale_copies]:
        copy.wait_send()


def finish(*refs):
    half = (len(refs) - 1) // 2
    sems = refs[-1]
    copies = [
        pltpu.make_async_copy(a, b, sems.at[i])
        for i, (a, b) in enumerate(zip(refs[:half], refs[half : 2 * half]))
    ]
    for copy in copies:
        copy.start()
    for copy in copies:
        copy.wait()


def body(radiances, band, row_in_band, column):
    nrows = lax.axis_size("rows")
    nchan = lax.axis_size("chan")
    fields, obs = radiances.shape
    cap = 2 * obs // nrows
    lines = cap // LANES
    npair = nchan // 2
    vmem = pl.BlockSpec(memory_space=pltpu.VMEM)
    anywhere = pl.BlockSpec(memory_space=pl.ANY)
    dma = pltpu.SemaphoreType.DMA
    shapes = (
        ((ROWS_DEV, COLS), jnp.int32),
        ((fields, ROWS_DEV, COLS), F32),
        ((fields, ROWS_DEV, COLS), F32),
        ((ROWS_DEV, COLS), F32),
        ((fields, obs), F32),
    )
    held = pl.pallas_call(
        functools.partial(kernel, nrows, nchan),
        out_shape=tuple(pltpu.VMEM(s, t) for s, t in shapes),
        in_specs=[pl.BlockSpec(memory_space=pltpu.HBM)] * 4,
        out_specs=(vmem,) * len(shapes),
        scratch_shapes=[
            pltpu.VMEM((fields, obs), F32),
            pltpu.VMEM((1, obs), jnp.int32),
            pltpu.VMEM((1, obs), jnp.int32),
            pltpu.VMEM((1, obs), jnp.int32),
            pltpu.VMEM((cap, obs), BF16),
            pltpu.VMEM((nrows * lines * 8, LANES), F32),
            pltpu.VMEM((nrows, fields + 1, lines, LANES), F32),
            pltpu.VMEM((nrows, fields + 1, lines, LANES), F32),
            pltpu.VMEM((fields, QS, LOW), F32),
            pltpu.VMEM((QS, LOW), F32),
            pltpu.VMEM((QS, LOW), F32),
            pltpu.VMEM((QS, LOW), F32),
            pltpu.VMEM((npair, QS, LOW), F32),
            pltpu.VMEM((nrows, fields, lines, LANES), F32),
            pltpu.VMEM((nrows, fields, lines, LANES), F32),
            pltpu.VMEM((nrows, lines, LANES), F32),
            pltpu.VMEM((npair * nrows, lines, LANES), F32),
            pltpu.VMEM((fields * obs // LANES, LANES), F32),
            pltpu.SemaphoreType.REGULAR,
            dma((4,)),
            dma((nrows,)),
            dma((nrows,)),
            dma((1,)),
            dma((1,)),
            dma((npair,)),
            dma((npair,)),
            dma((nrows,)),
            dma((nrows,)),
            dma((npair * nrows,)),
            dma((npair * nrows,)),
        ],
        compiler_params=pltpu.CompilerParams(
            collective_id=0, has_side_effects=True, vmem_limit_bytes=32 * 1024 * 1024
        ),
    )(
        *(
            pltpu.with_memory_space_constraint(x, pltpu.HBM)
            for x in (
                radiances,
                band.reshape(1, obs),
                row_in_band.reshape(1, obs),
                column.reshape(1, obs),
            )
        )
    )
    return pl.pallas_call(
        finish,
        out_shape=tuple(jax.ShapeDtypeStruct(s, t) for s, t in shapes),
        in_specs=[vmem] * len(shapes),
        out_specs=(anywhere,) * len(shapes),
        scratch_shapes=[dma((len(shapes),))],
        compiler_params=pltpu.CompilerParams(vmem_limit_bytes=32 * 1024 * 1024),
    )(*held)


def solution(mesh):
    in_specs = (P("chan", "rows"), P("rows", None), P("rows"), P("rows"))
    out_specs = (
        P("rows", None),
        P("chan", "rows", None),
        P("chan", "rows", None),
        P("rows", None),
        P("chan", "rows"),
    )
    return jax.shard_map(body, mesh=mesh, in_specs=in_specs, out_specs=out_specs, check_vma=False)
```

time: 20.4 us -> 20 us (0.980)
  Pallas kernels: 19.5 us -> 19.1 us
    pallas_call x1, Pallas kernels: 1.38 us -> 0.74 us  [body(): pl.pallas_call(finish, out_shape=tuple((jax.ShapeDtypeStruct(s, t) for s,...]
    pallas_call x1, Pallas kernels: 18.1 us -> 18.4 us  [body(): pl.pallas_call(functools.partial(kernel, nrows, nchan), out_shape=tuple((...]
where the time goes in v1:
time: 20 us; the launch traced here: 19.7 us
  Pallas kernels  19.1 us (96%)
  between operations  0.64 us (3%)
    pallas_call x1, Pallas kernels, body(): pl.pallas_call(functools.partial(kernel, nrows, nchan), out_shape=tuple((...  18.4 us
    pallas_call x1, Pallas kernels, body(): pl.pallas_call(finish, out_shape=tuple((jax.ShapeDtypeStruct(s, t) for s,...  0.74 us

profile of v1, /device:TPU:0, one launch (start us, length us, event | category | flops | bytes accessed | tf_op | source)
XLA Modules:
  0.0 19.7 jit_solution(6870524580924216363)
XLA Ops:
  0.6 18.4 %shard_map.83 = (s32[4,1440]{1,0:T(4,128)S(1)}, f32[4,4,1440]{2,1,0:T(4,128)S(1)}, f32[4,4,1440]{2,1,0:T(4,128)S(1)}, f32[4,1440]{1,0:T(4,128)S(1)}, f32[4,2048]{1,0:T(4,128)S(1)}) custom-call(f32[4,2048]{1,0:T(4,128)} %rad_in.1, s32[1,2048]{1,0:T(1,128)} %bitcast.3, s32[1,2048]{1,0:T(1,128)} %bitcast.4, s32[1,2048]{1,0:T(1,128)} %bitcast.5), custom_call_target="tpu_custom_call" | custom-call | tf_op jit(solution)/shard_map/pallas_call | solution.py:411
  19.0 0.7 %shard_map.84 = (s32[4,1440]{1,0:T(4,128)}, f32[4,4,1440]{2,1,0:T(4,128)}, f32[4,4,1440]{2,1,0:T(4,128)}, f32[4,1440]{1,0:T(4,128)}, f32[4,2048]{1,0:T(4,128)}) custom-call(s32[4,1440]{1,0:T(4,128)S(1)} %get-tuple-element.10.refs_0_, f32[4,4,1440]{2,1,0:T(4,128)S(1)} %get-tuple-element.11.refs_1_, f32[4,4,1440]{2,1,0:T(4,128)S(1)} %get-tuple-element.12.refs_2_, ...), custom_call_target="tpu_custom_call" | custom-call | tf_op jit(solution)/shard_map/pallas_call | solution.py:462

commit v2 on v1

v2 whole, which is shorter than its diff:
```python
import functools

import jax
import jax.numpy as jnp
from jax import lax
from jax.experimental import pallas as pl
from jax.experimental.pallas import tpu as pltpu
from jax.sharding import PartitionSpec as P

CHAN = 16
PACK = 16
COLS = 1440
ROWS_DEV = 4
LOW = 256
LANES = 128
BLOCKS = -(-COLS // LOW)
QS = BLOCKS * ROWS_DEV
F32 = jnp.float32
BF16 = jnp.bfloat16
MESH = pl.DeviceIdType.MESH
NT = (((1,), (1,)), ((), ()))
NN = (((1,), (0,)), ((), ()))


def iota(shape, axis):
    return lax.broadcasted_iota(jnp.int32, shape, axis)


def onehot(mask):
    return jnp.where(mask, 1.0, 0.0)


def two(values):
    high = values.astype(BF16).astype(F32)
    return high, values - high


def product(accs, tiles, transpose):
    for i in range(0, len(tiles), 2):
        pair = tiles[i : i + 2]
        if len(pair) < 2:
            pair.append([jnp.zeros_like(x) for x in pair[0]])
        left, right = (jnp.concatenate(x, axis=1) for x in zip(*pair))
        unit, register = i // 2 % 2, i // 4 % 2
        pltpu.matmul_push_rhs(
            right, staging_register=register, mxu_index=unit, transpose=transpose
        )
        pltpu.matmul_acc_lhs(accs[unit], left, load_staged_rhs=register)


def flip(index, bits):
    out, bit = index, 1
    while bit <= bits:
        if bits & bit:
            out = out + bit - 2 * bit * ((index // bit) % 2)
        bit *= 2
    return out


def rank_of(dest, nrows, acc):
    obs = dest.shape[1]
    nblock = obs // LOW
    hot = [
        onehot(iota((nrows, LOW), 0) == dest[:, b * LOW : (b + 1) * LOW]) for b in range(nblock)
    ]
    upper = onehot(iota((LOW, LOW), 0) < iota((LOW, LOW), 1)).astype(BF16)
    pltpu.matmul_push_rhs(upper, staging_register=0, mxu_index=0)
    pltpu.matmul_acc_lhs(acc, jnp.concatenate(hot, axis=0).astype(BF16), load_staged_rhs=0)
    inner = pltpu.matmul_pop(acc)
    rows, before = [], None
    for b in range(nblock):
        count = inner[b * nrows : (b + 1) * nrows]
        if before is not None:
            count = count + before
        row = jnp.sum(hot[b] * count, axis=0, keepdims=True)
        rows += [row[:, k : k + LANES] for k in range(0, LOW, LANES)]
        size = jnp.sum(hot[b], axis=1, keepdims=True)
        before = size if before is None else before + size
    return rows


def spill(out, values):
    for j in range(BLOCKS):
        start = j * LOW
        width = min(LOW, COLS - start)
        out[:, start : start + width] = values[j * ROWS_DEV : (j + 1) * ROWS_DEV, :width].astype(
            out.dtype
        )


def folded(row):
    lines = row.shape[1] // LANES
    return jnp.concatenate([row[:, k * LANES : (k + 1) * LANES] for k in range(lines)], axis=0)


def take(row, lane):
    return jnp.take_along_axis(
        jnp.broadcast_to(row, lane.shape), lane, axis=1, mode="promise_in_bounds"
    )


def packed(row):
    return jnp.broadcast_to(row, (PACK, row.shape[1])).astype(BF16)


def steps(first, period=PACK):
    return (iota((PACK, LANES), 0) % period + first).astype(F32).astype(BF16)


def low_hot(row, size):
    wide = packed(row)
    one, zero = jnp.ones((PACK, LANES), BF16), jnp.zeros((PACK, LANES), BF16)
    return jnp.concatenate(
        [jnp.where(steps(b) == wide, one, zero) for b in range(0, size, PACK)], axis=0
    )


def tiles_of(arrived, col_hot, slots):
    fields, lines = arrived.shape[1] - 1, arrived.shape[2]
    one, zero = jnp.ones((PACK, LANES), BF16), jnp.zeros((PACK, LANES), BF16)
    tiles = []
    for d in slots:
        cells = arrived[d, fields]
        high = jnp.floor(cells * (1.0 / LOW))
        low, high = cells - high * LOW, high - 1.0
        features = []
        for f in range(fields):
            x = arrived[d, f]
            features += [two(x), two(x * x)]
        for t in range(lines):
            hot = low_hot(low[t : t + 1], LOW)
            col_hot[d, :, t * LANES : (t + 1) * LANES] = hot
            quad = packed(high[t : t + 1])
            pairs = [
                jnp.concatenate(
                    [jnp.broadcast_to(x[t : t + 1], (8, LANES)) for x in feature], axis=0
                ).astype(BF16)
                for feature in features
            ]
            rows = []
            for j in range(0, QS, 8):
                here = steps(j, 8) == quad
                rows += [jnp.where(here, x, zero) for x in pairs]
            for j in range(0, QS, PACK):
                rows.append(jnp.where(steps(j) == quad, one, zero))
            tiles.append([jnp.concatenate(rows, axis=0), hot])
    return tiles


def grids_of(total, fields):
    out = []
    for p in range(2 * fields):
        rows = []
        for j in range(QS // 8):
            at = (j * 2 * fields + p) * 16
            rows.append(total[at : at + 8] + total[at + 8 : at + 16])
        out.append(jnp.concatenate(rows, axis=0))
    at = QS // 8 * 2 * fields * 16
    return total[at : at + QS], out[0::2], out[1::2]


def kernel(
    nrows,
    nchan,
    rad_in,
    band_in,
    rib_in,
    col_in,
    cnt_out,
    mean_out,
    var_out,
    spr_out,
    dep_out,
    rad_ref,
    band_ref,
    rib_ref,
    col_ref,
    staged,
    sent,
    arrived,
    col_hot,
    part_s,
    part_r,
    pairs,
    share_s,
    share_r,
    back_s,
    back_r,
    scale_s,
    scale_r,
    turned,
    ready,
    ins,
    so,
    ro,
    sp,
    rp,
    sh,
    rh,
    sg,
    rg,
    sb,
    rb,
    ss,
    rs,
):
    me = lax.axis_index("rows")
    mc = lax.axis_index("chan")
    fields, obs = rad_ref.shape
    cap = 2 * obs // nrows
    lines = cap // LANES
    npair = nchan // 2
    far = list(range(nrows - 1, 0, -1))
    row_peer = [flip(me, d) for d in range(nrows)]
    chan_peer = [lax.rem(mc + 2 * j, nchan) for j in range(npair)]
    partner = flip(mc, 1)

    def remote(src, dst, send, recv, **to):
        return pltpu.make_async_remote_copy(
            src_ref=src,
            dst_ref=dst,
            send_sem=send,
            recv_sem=recv,
            device_id=to,
            device_id_type=MESH,
        )

    barrier = pltpu.get_barrier_semaphore()
    for d in far:
        pl.semaphore_signal(
            barrier, inc=1, device_id={"rows": row_peer[d]}, device_id_type=MESH
        )
    for peer in chan_peer[1:] + [partner]:
        pl.semaphore_signal(barrier, inc=1, device_id={"chan": peer}, device_id_type=MESH)
    fetches = [
        pltpu.make_async_copy(a, b, ins.at[i])
        for i, (a, b) in enumerate(
            ((band_in, band_ref), (rad_in, rad_ref), (rib_in, rib_ref), (col_in, col_ref))
        )
    ]
    for fetch in fetches:
        fetch.start()

    fetches[0].wait()
    dest = band_ref[...]

    def place_all(acc_rank, *accs):
        ranks = rank_of(dest, nrows, acc_rank)
        rank = folded(jnp.concatenate(ranks, axis=1)).astype(jnp.int32)
        wide = min(cap, LOW)
        parts = cap // wide
        hots, keys = [], []
        for k in range(obs // LANES):
            upper = jnp.floor(ranks[k] * (1.0 / wide))
            hots.append(low_hot(ranks[k] - upper * wide, LOW))
            names = jnp.bitwise_xor(dest[:, k * LANES : (k + 1) * LANES], me)
            keys.append(packed(names.astype(F32) * parts + upper))
        for fetch in fetches[1:]:
            fetch.wait()
        high, rest = two(rad_ref[...])
        middle, low = two(rest)
        col = col_ref[...]
        code = (col // LOW) * ROWS_DEV + rib_ref[...] + 1
        payload = jnp.concatenate(
            [high, middle, low]
            + [code.astype(F32), (col & (LOW - 1)).astype(F32)]
            + [jnp.zeros((PACK - 3 * fields - 2, obs), F32)],
            axis=0,
        ).astype(BF16)
        zero = jnp.zeros((PACK, LANES), BF16)
        left = []
        for k in range(obs // LANES):
            load = payload[:, k * LANES : (k + 1) * LANES]
            left.append(
                jnp.concatenate(
                    [
                        jnp.where(keys[k] == jnp.full((PACK, LANES), key, BF16), load, zero)
                        for key in range(nrows * parts)
                    ],
                    axis=0,
                )
            )
        product(accs, [list(x) for x in zip(left, hots)], True)
        placed = pltpu.matmul_pop(accs[0]) + pltpu.matmul_pop(accs[1])
        for d in far + [0]:
            target = sent if d > 0 else arrived
            for p in range(parts):
                part = placed[(d * parts + p) * PACK : (d * parts + p + 1) * PACK]
                values = (part[:fields] + part[fields : 2 * fields]) + part[2 * fields : 3 * fields]
                cells = part[3 * fields : 3 * fields + 1] * LOW + part[3 * fields + 1 : 3 * fields + 2]
                for i in range(wide // LANES):
                    t = p * (wide // LANES) + i
                    span = slice(i * LANES, (i + 1) * LANES)
                    at = (d * lines + t) * 8
                    staged[at : at + fields] = values[:, span]
                    staged[at + fields : at + fields + 1] = cells[:, span]
            for f in range(fields + 1):
                target[d, f] = staged[pl.ds(d * lines * 8 + f, lines, stride=8), :]
        return rank

    rows_placed = nrows * max(1, cap // LOW) * PACK
    rank = pl.run_scoped(
        place_all,
        pltpu.ACC(0)((nrows * obs // LOW, LOW), F32),
        pltpu.ACC(0)((rows_placed, LOW), F32),
        pltpu.ACC(1)((rows_placed, LOW), F32),
    )
    pl.semaphore_wait(barrier, nrows - 1 + npair)
    out_copies = {}
    for d in far:
        out_copies[d] = remote(
            sent.at[d], arrived.at[d], so.at[d], ro.at[d], rows=row_peer[d]
        )
        out_copies[d].start()
    for j in range(1, npair):
        pl.semaphore_signal(ready, inc=1, device_id={"chan": chan_peer[j]}, device_id_type=MESH)

    half_rows = nrows // 2
    back_copies, share_copies = {}, {}

    def cells_all(acc_0, acc_1, *looks):
        accs = (acc_0, acc_1)
        groups = [[0], list(range(1, half_rows)), list(range(half_rows, nrows))]
        for slots in groups:
            for d in slots:
                if d > 0:
                    out_copies[d].wait_recv()
            product(accs, tiles_of(arrived, col_hot, slots), True)

        total = pltpu.matmul_pop(accs[0]) + pltpu.matmul_pop(accs[1])
        count, firsts, seconds = grids_of(total, fields)
        inverse = 1.0 / jnp.maximum(count, 1.0)
        partial = None
        means, variances = [], []
        for f in range(fields):
            mean = firsts[f] * inverse
            variance = jnp.maximum(seconds[f] * inverse - mean * mean, 0.0)
            means.append(mean)
            variances.append(variance)
            partial = variance if partial is None else partial + variance

        split = [two(x) for x in means + [partial]]
        pad = jnp.zeros((-(fields + 1) * QS % PACK, LOW), F32)
        table = [jnp.concatenate([x[k] for x in split] + [pad], axis=0).astype(BF16) for k in (0, 1)]
        places = [(d, t) for d in far + [0] for t in range(lines)]
        for i in range(0, len(places), 2):
            unit, ring = i // 2 % 2, i // 4 % 2
            acc = looks[unit * 2 + ring]
            hot = jnp.concatenate(
                [col_hot[d, :, t * LANES : (t + 1) * LANES] for d, t in places[i : i + 2]], axis=1
            )
            pltpu.matmul_push_rhs(hot, staging_register=ring, mxu_index=unit)
            pltpu.matmul_acc_lhs(acc, table[0], load_staged_rhs=ring)
            pltpu.matmul_acc_lhs(acc, table[1])
            picked = pltpu.matmul_pop(acc)
            for k, (d, t) in enumerate(places[i : i + 2]):
                span = slice(k * LANES, (k + 1) * LANES)
                target = back_s if d > 0 else back_r
                high = arrived[d, fields, t : t + 1].astype(jnp.int32) // LOW - 1
                here = iota((QS, LANES), 0) == high
                for f in range(fields + 1):
                    both = picked[f * QS : (f + 1) * QS, span]
                    found = jnp.sum(jnp.where(here, both, 0.0), axis=0, keepdims=True)
                    if f < fields:
                        target[d, f, t : t + 1] = arrived[d, f, t : t + 1] - found
                    else:
                        share_s[d, t : t + 1] = found
                if t < lines - 1:
                    continue
                share_copies[d] = remote(
                    share_s.at[d], share_r.at[d], sh.at[d], rh.at[d], chan=partner
                )
                share_copies[d].start()
                if d > 0:
                    back_copies[d] = remote(
                        back_s.at[d], back_r.at[d], sb.at[d], rb.at[d], rows=row_peer[d]
                    )
                    back_copies[d].start()
        part_s[...] = partial
        part_copy = remote(part_s, part_r, sp.at[0], rp.at[0], chan=partner)
        part_copy.start()

        spill(cnt_out, count)
        for f in range(fields):
            spill(mean_out.at[f], means[f])
            spill(var_out.at[f], variances[f])
        pl.semaphore_wait(ready, npair - 1)
        scale_copies = []
        for d in far + [0]:
            share_copies[d].wait_recv()
            scale_s[d] = share_s[d] + share_r[d]
            if d == 0:
                scale_r[0] = share_s[d] + share_r[d]
            for j in list(range(1, npair)) + [0]:
                if d + j == 0:
                    continue
                slot = j * nrows + d
                copy = remote(
                    scale_s.at[d],
                    scale_r.at[slot],
                    ss.at[slot],
                    rs.at[slot],
                    rows=row_peer[d],
                    chan=chan_peer[j],
                )
                copy.start()
                scale_copies.append((d, copy))
        part_copy.wait_recv()
        mine = mc // 2
        pairs[mine] = part_s[...] + part_r[...]
        pair_copies = []
        for j in range(1, npair):
            copy = remote(pairs.at[mine], pairs.at[mine], sg.at[j], rg.at[j], chan=chan_peer[j])
            copy.start()
            pair_copies.append(copy)

        place = jnp.bitwise_xor(folded(dest), me) * lines + rank // LANES
        lane = rank & (LANES - 1)
        found = [jnp.zeros(rank.shape, F32) for _ in range(fields + 1)]
        far_half = list(range(nrows - 1, half_rows - 1, -1))
        returns = [list(range(half_rows)), far_half]
        for slots in returns:
            for d in slots:
                if d > 0:
                    back_copies[d].wait_recv()
            for d in slots:
                for t in range(lines):
                    here = place == d * lines + t
                    for f in range(fields):
                        found[f] = jnp.where(here, take(back_r[d, f, t : t + 1], lane), found[f])
        for slots in returns:
            for d, copy in scale_copies:
                if d in slots:
                    copy.wait_recv()
            for d in slots:
                for t in range(lines):
                    here = place == d * lines + t
                    row = scale_r[d, t : t + 1]
                    for j in range(1, npair):
                        row = row + scale_r[j * nrows + d, t : t + 1]
                    found[fields] = jnp.where(here, take(row, lane), found[fields])
        scale = lax.rsqrt(1.0 + found[fields] / CHAN)
        many = obs // LANES
        for f in range(fields):
            turned[f * many : (f + 1) * many] = found[f] * scale
        for k in range(many):
            dep_out[:, k * LANES : (k + 1) * LANES] = turned[pl.ds(k, fields, stride=many), :]
        for copy in pair_copies:
            copy.wait_recv()
        spread = pairs[0]
        for p in range(1, npair):
            spread = spread + pairs[p]
        spill(spr_out, spread)

        for copies in (out_copies, back_copies, share_copies):
            for copy in copies.values():
                copy.wait_send()
        for copy in [part_copy] + pair_copies + [copy for _, copy in scale_copies]:
            copy.wait_send()

    rows_summed = QS * 4 * fields + -(-QS // PACK) * PACK
    rows_looked = -(-(fields + 1) * QS // PACK) * PACK
    pl.run_scoped(
        cells_all,
        *(pltpu.ACC(unit)((rows_summed, LOW), F32) for unit in (0, 1)),
        *(pltpu.ACC(unit)((rows_looked, LOW), F32) for unit in (0, 0, 1, 1)),
    )


def finish(*refs):
    half = (len(refs) - 1) // 2
    sems = refs[-1]
    copies = [
        pltpu.make_async_copy(a, b, sems.at[i])
        for i, (a, b) in enumerate(zip(refs[:half], refs[half : 2 * half]))
    ]
    for copy in copies:
        copy.start()
    for copy in copies:
        copy.wait()


def body(radiances, band, row_in_band, column):
    nrows = lax.axis_size("rows")
    nchan = lax.axis_size("chan")
    fields, obs = radiances.shape
    cap = 2 * obs // nrows
    lines = cap // LANES
    npair = nchan // 2
    vmem = pl.BlockSpec(memory_space=pltpu.VMEM)
    anywhere = pl.BlockSpec(memory_space=pl.ANY)
    dma = pltpu.SemaphoreType.DMA
    shapes = (
        ((ROWS_DEV, COLS), jnp.int32),
        ((fields, ROWS_DEV, COLS), F32),
        ((fields, ROWS_DEV, COLS), F32),
        ((ROWS_DEV, COLS), F32),
        ((fields, obs), F32),
    )
    held = pl.pallas_call(
        functools.partial(kernel, nrows, nchan),
        out_shape=tuple(pltpu.VMEM(s, t) for s, t in shapes),
        in_specs=[pl.BlockSpec(memory_space=pltpu.HBM)] * 4,
        out_specs=(vmem,) * len(shapes),
        scratch_shapes=[
            pltpu.VMEM((fields, obs), F32),
            pltpu.VMEM((1, obs), jnp.int32),
            pltpu.VMEM((1, obs), jnp.int32),
            pltpu.VMEM((1, obs), jnp.int32),
            pltpu.VMEM((nrows * lines * 8, LANES), F32),
            pltpu.VMEM((nrows, fields + 1, lines, LANES), F32),
            pltpu.VMEM((nrows, fields + 1, lines, LANES), F32),
            pltpu.VMEM((nrows, LOW, cap), BF16),
            pltpu.VMEM((QS, LOW), F32),
            pltpu.VMEM((QS, LOW), F32),
            pltpu.VMEM((npair, QS, LOW), F32),
            pltpu.VMEM((nrows, lines, LANES), F32),
            pltpu.VMEM((nrows, lines, LANES), F32),
            pltpu.VMEM((nrows, fields, lines, LANES), F32),
            pltpu.VMEM((nrows, fields, lines, LANES), F32),
            pltpu.VMEM((nrows, lines, LANES), F32),
            pltpu.VMEM((npair * nrows, lines, LANES), F32),
            pltpu.VMEM((fields * obs // LANES, LANES), F32),
            pltpu.SemaphoreType.REGULAR,
            dma((4,)),
            dma((nrows,)),
            dma((nrows,)),
            dma((1,)),
            dma((1,)),
            dma((nrows,)),
            dma((nrows,)),
            dma((npair,)),
            dma((npair,)),
            dma((nrows,)),
            dma((nrows,)),
            dma((npair * nrows,)),
            dma((npair * nrows,)),
        ],
        compiler_params=pltpu.CompilerParams(
            collective_id=0, has_side_effects=True, vmem_limit_bytes=32 * 1024 * 1024
        ),
    )(
        *(
            pltpu.with_memory_space_constraint(x, pltpu.HBM)
            for x in (
                radiances,
                band.reshape(1, obs),
                row_in_band.reshape(1, obs),
                column.reshape(1, obs),
            )
        )
    )
    return pl.pallas_call(
        finish,
        out_shape=tuple(jax.ShapeDtypeStruct(s, t) for s, t in shapes),
        in_specs=[vmem] * len(shapes),
        out_specs=(anywhere,) * len(shapes),
        scratch_shapes=[dma((len(shapes),))],
        compiler_params=pltpu.CompilerParams(vmem_limit_bytes=32 * 1024 * 1024),
    )(*held)


def solution(mesh):
    in_specs = (P("chan", "rows"), P("rows", None), P("rows"), P("rows"))
    out_specs = (
        P("rows", None),
        P("chan", "rows", None),
        P("chan", "rows", None),
        P("rows", None),
        P("chan", "rows"),
    )
    return jax.shard_map(body, mesh=mesh, in_specs=in_specs, out_specs=out_specs, check_vma=False)
```

time: 20 us -> 20.1 us (level)
  no operation moved by 1% of the time
where the time goes in v2:
time: 20.1 us; the launch traced here: 19.9 us
  Pallas kernels  19.3 us (96%)
  between operations  0.64 us (3%)
    pallas_call x1, Pallas kernels, body(): pl.pallas_call(functools.partial(kernel, nrows, nchan), out_shape=tuple((...  18.5 us
    pallas_call x1, Pallas kernels, body(): pl.pallas_call(finish, out_shape=tuple((jax.ShapeDtypeStruct(s, t) for s,...  0.74 us

profile of v2, /device:TPU:0, one launch (start us, length us, event | category | flops | bytes accessed | tf_op | source)
XLA Modules:
  0.0 19.9 jit_solution(7542701201426981918)
XLA Ops:
  0.6 18.5 %shard_map.83 = (s32[4,1440]{1,0:T(4,128)S(1)}, f32[4,4,1440]{2,1,0:T(4,128)S(1)}, f32[4,4,1440]{2,1,0:T(4,128)S(1)}, f32[4,1440]{1,0:T(4,128)S(1)}, f32[4,2048]{1,0:T(4,128)S(1)}) custom-call(f32[4,2048]{1,0:T(4,128)} %rad_in.1, s32[1,2048]{1,0:T(1,128)} %bitcast.3, s32[1,2048]{1,0:T(1,128)} %bitcast.4, s32[1,2048]{1,0:T(1,128)} %bitcast.5), custom_call_target="tpu_custom_call" | custom-call | tf_op jit(solution)/shard_map/pallas_call | solution.py:500
  19.2 0.7 %shard_map.84 = (s32[4,1440]{1,0:T(4,128)}, f32[4,4,1440]{2,1,0:T(4,128)}, f32[4,4,1440]{2,1,0:T(4,128)}, f32[4,1440]{1,0:T(4,128)}, f32[4,2048]{1,0:T(4,128)}) custom-call(s32[4,1440]{1,0:T(4,128)S(1)} %get-tuple-element.10.refs_0_, f32[4,4,1440]{2,1,0:T(4,128)S(1)} %get-tuple-element.11.refs_1_, f32[4,4,1440]{2,1,0:T(4,128)S(1)} %get-tuple-element.12.refs_2_, ...), custom_call_target="tpu_custom_call" | custom-call | tf_op jit(solution)/shard_map/pallas_call | solution.py:553

commit v3 on v2

--- a/solution.py
+++ b/solution.py
@@ -182,11 +182,8 @@
     part_s,
     part_r,
     pairs,
-    share_s,
-    share_r,
     back_s,
     back_r,
-    scale_s,
     scale_r,
     turned,
     ready,
@@ -195,8 +192,6 @@
     ro,
     sp,
     rp,
-    sh,
-    rh,
     sg,
     rg,
     sb,
@@ -230,8 +225,8 @@
         pl.semaphore_signal(
             barrier, inc=1, device_id={"rows": row_peer[d]}, device_id_type=MESH
         )
-    for peer in chan_peer[1:] + [partner]:
-        pl.semaphore_signal(barrier, inc=1, device_id={"chan": peer}, device_id_type=MESH)
+    for e in range(1, nchan):
+        pl.semaphore_signal(barrier, inc=1, device_id={"chan": flip(mc, e)}, device_id_type=MESH)
     fetches = [
         pltpu.make_async_copy(a, b, ins.at[i])
         for i, (a, b) in enumerate(
@@ -305,18 +300,18 @@
         pltpu.ACC(0)((rows_placed, LOW), F32),
         pltpu.ACC(1)((rows_placed, LOW), F32),
     )
-    pl.semaphore_wait(barrier, nrows - 1 + npair)
+    pl.semaphore_wait(barrier, nrows + nchan - 2)
     out_copies = {}
     for d in far:
         out_copies[d] = remote(
             sent.at[d], arrived.at[d], so.at[d], ro.at[d], rows=row_peer[d]
         )
         out_copies[d].start()
-    for j in range(1, npair):
-        pl.semaphore_signal(ready, inc=1, device_id={"chan": chan_peer[j]}, device_id_type=MESH)
+    for e in range(1, nchan):
+        pl.semaphore_signal(ready, inc=1, device_id={"chan": flip(mc, e)}, device_id_type=MESH)
 
     half_rows = nrows // 2
-    back_copies, share_copies = {}, {}
+    back_copies = {}
 
     def cells_all(acc_0, acc_1, *looks):
         accs = (acc_0, acc_1)
@@ -343,17 +338,27 @@
         pad = jnp.zeros((-(fields + 1) * QS % PACK, LOW), F32)
         table = [jnp.concatenate([x[k] for x in split] + [pad], axis=0).astype(BF16) for k in (0, 1)]
         places = [(d, t) for d in far + [0] for t in range(lines)]
-        for i in range(0, len(places), 2):
-            unit, ring = i // 2 % 2, i // 4 % 2
-            acc = looks[unit * 2 + ring]
+        tiles = [places[i : i + 2] for i in range(0, len(places), 2)]
+
+        def issue(i):
+            register = i // 2 % 2
             hot = jnp.concatenate(
-                [col_hot[d, :, t * LANES : (t + 1) * LANES] for d, t in places[i : i + 2]], axis=1
+                [col_hot[d, :, t * LANES : (t + 1) * LANES] for d, t in tiles[i]], axis=1
             )
-            pltpu.matmul_push_rhs(hot, staging_register=ring, mxu_index=unit)
-            pltpu.matmul_acc_lhs(acc, table[0], load_staged_rhs=ring)
+            acc = looks[i % len(looks)]
+            pltpu.matmul_push_rhs(hot, staging_register=register, mxu_index=i % 2)
+            pltpu.matmul_acc_lhs(acc, table[0], load_staged_rhs=register)
             pltpu.matmul_acc_lhs(acc, table[1])
-            picked = pltpu.matmul_pop(acc)
-            for k, (d, t) in enumerate(places[i : i + 2]):
+
+        pl.semaphore_wait(ready, nchan - 1)
+        scale_copies = []
+        for i in range(min(len(looks), len(tiles))):
+            issue(i)
+        for i, tile in enumerate(tiles):
+            picked = pltpu.matmul_pop(looks[i % len(looks)])
+            if i + len(looks) < len(tiles):
+                issue(i + len(looks))
+            for k, (d, t) in enumerate(tile):
                 span = slice(k * LANES, (k + 1) * LANES)
                 target = back_s if d > 0 else back_r
                 high = arrived[d, fields, t : t + 1].astype(jnp.int32) // LOW - 1
@@ -364,13 +369,21 @@
                     if f < fields:
                         target[d, f, t : t + 1] = arrived[d, f, t : t + 1] - found
                     else:
-                        share_s[d, t : t + 1] = found
+                        target[d, f, t : t + 1] = found
                 if t < lines - 1:
                     continue
-                share_copies[d] = remote(
-                    share_s.at[d], share_r.at[d], sh.at[d], rh.at[d], chan=partner
-                )
-                share_copies[d].start()
+                for e in range(nchan - 1, 0, -1):
+                    slot = e * nrows + d
+                    copy = remote(
+                        target.at[d, fields],
+                        scale_r.at[slot],
+                        ss.at[slot],
+                        rs.at[slot],
+                        rows=row_peer[d],
+                        chan=flip(mc, e),
+                    )
+                    copy.start()
+                    scale_copies.append((d, copy))
                 if d > 0:
                     back_copies[d] = remote(
                         back_s.at[d], back_r.at[d], sb.at[d], rb.at[d], rows=row_peer[d]
@@ -384,27 +397,6 @@
         for f in range(fields):
             spill(mean_out.at[f], means[f])
             spill(var_out.at[f], variances[f])
-        pl.semaphore_wait(ready, npair - 1)
-        scale_copies = []
-        for d in far + [0]:
-            share_copies[d].wait_recv()
-            scale_s[d] = share_s[d] + share_r[d]
-            if d == 0:
-                scale_r[0] = share_s[d] + share_r[d]
-            for j in list(range(1, npair)) + [0]:
-                if d + j == 0:
-                    continue
-                slot = j * nrows + d
-                copy = remote(
-                    scale_s.at[d],
-                    scale_r.at[slot],
-                    ss.at[slot],
-                    rs.at[slot],
-                    rows=row_peer[d],
-                    chan=chan_peer[j],
-                )
-                copy.start()
-                scale_copies.append((d, copy))
         part_copy.wait_recv()
         mine = mc // 2
         pairs[mine] = part_s[...] + part_r[...]
@@ -435,9 +427,9 @@
             for d in slots:
                 for t in range(lines):
                     here = place == d * lines + t
-                    row = scale_r[d, t : t + 1]
-                    for j in range(1, npair):
-                        row = row + scale_r[j * nrows + d, t : t + 1]
+                    row = back_r[d, fields, t : t + 1]
+                    for e in range(1, nchan):
+                        row = row + scale_r[e * nrows + d, t : t + 1]
                     found[fields] = jnp.where(here, take(row, lane), found[fields])
         scale = lax.rsqrt(1.0 + found[fields] / CHAN)
         many = obs // LANES
@@ -452,7 +444,7 @@
             spread = spread + pairs[p]
         spill(spr_out, spread)
 
-        for copies in (out_copies, back_copies, share_copies):
+        for copies in (out_copies, back_copies):
             for copy in copies.values():
                 copy.wait_send()
         for copy in [part_copy] + pair_copies + [copy for _, copy in scale_copies]:
@@ -463,7 +455,7 @@
     pl.run_scoped(
         cells_all,
         *(pltpu.ACC(unit)((rows_summed, LOW), F32) for unit in (0, 1)),
-        *(pltpu.ACC(unit)((rows_looked, LOW), F32) for unit in (0, 0, 1, 1)),
+        *(pltpu.ACC(unit)((rows_looked, LOW), F32) for unit in (0, 1) * 4),
     )
 
 
@@ -514,12 +506,9 @@
             pltpu.VMEM((QS, LOW), F32),
             pltpu.VMEM((QS, LOW), F32),
             pltpu.VMEM((npair, QS, LOW), F32),
-            pltpu.VMEM((nrows, lines, LANES), F32),
-            pltpu.VMEM((nrows, lines, LANES), F32),
-            pltpu.VMEM((nrows, fields, lines, LANES), F32),
-            pltpu.VMEM((nrows, fields, lines, LANES), F32),
-            pltpu.VMEM((nrows, lines, LANES), F32),
-            pltpu.VMEM((npair * nrows, lines, LANES), F32),
+            pltpu.VMEM((nrows, fields + 1, lines, LANES), F32),
+            pltpu.VMEM((nrows, fields + 1, lines, LANES), F32),
+            pltpu.VMEM((nchan * nrows, lines, LANES), F32),
             pltpu.VMEM((fields * obs // LANES, LANES), F32),
             pltpu.SemaphoreType.REGULAR,
             dma((4,)),
@@ -527,14 +516,12 @@
             dma((nrows,)),
             dma((1,)),
             dma((1,)),
-            dma((nrows,)),
-            dma((nrows,)),
             dma((npair,)),
             dma((npair,)),
             dma((nrows,)),
             dma((nrows,)),
-            dma((npair * nrows,)),
-            dma((npair * nrows,)),
+            dma((nchan * nrows,)),
+            dma((nchan * nrows,)),
         ],
         compiler_params=pltpu.CompilerParams(
             collective_id=0, has_side_effects=True, vmem_limit_bytes=32 * 1024 * 1024

time: 20.1 us -> 18.7 us (0.930)
  Pallas kernels: 19.3 us -> 17.9 us
    pallas_call x1, Pallas kernels: 18.5 us -> 17.1 us  [body(): pl.pallas_call(functools.partial(kernel, nrows, nchan), out_shape=tuple((...]
where the time goes in v3:
time: 18.7 us; the launch traced here: 18.5 us
  Pallas kernels  17.9 us (96%)
  between operations  0.64 us (3%)
    pallas_call x1, Pallas kernels, body(): pl.pallas_call(functools.partial(kernel, nrows, nchan), out_shape=tuple((...  17.1 us
    pallas_call x1, Pallas kernels, body(): pl.pallas_call(finish, out_shape=tuple((jax.ShapeDtypeStruct(s, t) for s,...  0.74 us

profile of v3, /device:TPU:0, one launch (start us, length us, event | category | flops | bytes accessed | tf_op | source)
XLA Modules:
  0.0 18.5 jit_solution(8294886285621552751)
XLA Ops:
  0.6 17.1 %shard_map.83 = (s32[4,1440]{1,0:T(4,128)S(1)}, f32[4,4,1440]{2,1,0:T(4,128)S(1)}, f32[4,4,1440]{2,1,0:T(4,128)S(1)}, f32[4,1440]{1,0:T(4,128)S(1)}, f32[4,2048]{1,0:T(4,128)S(1)}) custom-call(f32[4,2048]{1,0:T(4,128)} %rad_in.1, s32[1,2048]{1,0:T(1,128)} %bitcast.3, s32[1,2048]{1,0:T(1,128)} %bitcast.4, s32[1,2048]{1,0:T(1,128)} %bitcast.5), custom_call_target="tpu_custom_call" | custom-call | tf_op jit(solution)/shard_map/pallas_call | solution.py:492
  17.8 0.7 %shard_map.84 = (s32[4,1440]{1,0:T(4,128)}, f32[4,4,1440]{2,1,0:T(4,128)}, f32[4,4,1440]{2,1,0:T(4,128)}, f32[4,1440]{1,0:T(4,128)}, f32[4,2048]{1,0:T(4,128)}) custom-call(s32[4,1440]{1,0:T(4,128)S(1)} %get-tuple-element.10.refs_0_, f32[4,4,1440]{2,1,0:T(4,128)S(1)} %get-tuple-element.11.refs_1_, f32[4,4,1440]{2,1,0:T(4,128)S(1)} %get-tuple-element.12.refs_2_, ...), custom_call_target="tpu_custom_call" | custom-call | tf_op jit(solution)/shard_map/pallas_call | solution.py:540

commit v4 on v3

--- a/solution.py
+++ b/solution.py
@@ -188,16 +188,11 @@
     turned,
     ready,
     ins,
-    so,
-    ro,
-    sp,
-    rp,
-    sg,
-    rg,
-    sb,
-    rb,
-    ss,
-    rs,
+    send,
+    came,
+    back,
+    scales,
+    shares,
 ):
     me = lax.axis_index("rows")
     mc = lax.axis_index("chan")
@@ -205,16 +200,20 @@
     cap = 2 * obs // nrows
     lines = cap // LANES
     npair = nchan // 2
+    half_rows = nrows // 2
     far = list(range(nrows - 1, 0, -1))
     row_peer = [flip(me, d) for d in range(nrows)]
     chan_peer = [lax.rem(mc + 2 * j, nchan) for j in range(npair)]
     partner = flip(mc, 1)
 
-    def remote(src, dst, send, recv, **to):
+    def wait_all(ref, semaphore):
+        pltpu.make_async_copy(ref, ref, semaphore).wait()
+
+    def remote(src, dst, kind, recv, **to):
         return pltpu.make_async_remote_copy(
             src_ref=src,
             dst_ref=dst,
-            send_sem=send,
+            send_sem=send.at[kind],
             recv_sem=recv,
             device_id=to,
             device_id_type=MESH,
@@ -301,25 +300,20 @@
         pltpu.ACC(1)((rows_placed, LOW), F32),
     )
     pl.semaphore_wait(barrier, nrows + nchan - 2)
-    out_copies = {}
     for d in far:
-        out_copies[d] = remote(
-            sent.at[d], arrived.at[d], so.at[d], ro.at[d], rows=row_peer[d]
-        )
-        out_copies[d].start()
+        remote(
+            sent.at[d], arrived.at[d], 0, came.at[d // half_rows], rows=row_peer[d]
+        ).start()
     for e in range(1, nchan):
         pl.semaphore_signal(ready, inc=1, device_id={"chan": flip(mc, e)}, device_id_type=MESH)
 
-    half_rows = nrows // 2
-    back_copies = {}
 
     def cells_all(acc_0, acc_1, *looks):
         accs = (acc_0, acc_1)
         groups = [[0], list(range(1, half_rows)), list(range(half_rows, nrows))]
         for slots in groups:
-            for d in slots:
-                if d > 0:
-                    out_copies[d].wait_recv()
+            if slots[0] > 0:
+                wait_all(arrived.at[slots[0] : slots[-1] + 1], came.at[slots[0] // half_rows])
             product(accs, tiles_of(arrived, col_hot, slots), True)
 
         total = pltpu.matmul_pop(accs[0]) + pltpu.matmul_pop(accs[1])
@@ -351,7 +345,6 @@
             pltpu.matmul_acc_lhs(acc, table[1])
 
         pl.semaphore_wait(ready, nchan - 1)
-        scale_copies = []
         for i in range(min(len(looks), len(tiles))):
             issue(i)
         for i, tile in enumerate(tiles):
@@ -374,23 +367,20 @@
                     continue
                 for e in range(nchan - 1, 0, -1):
                     slot = e * nrows + d
-                    copy = remote(
+                    remote(
                         target.at[d, fields],
                         scale_r.at[slot],
-                        ss.at[slot],
-                        rs.at[slot],
+                        2,
+                        scales.at[d // half_rows],
                         rows=row_peer[d],
                         chan=flip(mc, e),
-                    )
-                    copy.start()
-                    scale_copies.append((d, copy))
+                    ).start()
                 if d > 0:
-                    back_copies[d] = remote(
-                        back_s.at[d], back_r.at[d], sb.at[d], rb.at[d], rows=row_peer[d]
-                    )
-                    back_copies[d].start()
+                    remote(
+                        back_s.at[d], back_r.at[d], 1, back.at[d // half_rows], rows=row_peer[d]
+                    ).start()
         part_s[...] = partial
-        part_copy = remote(part_s, part_r, sp.at[0], rp.at[0], chan=partner)
+        part_copy = remote(part_s, part_r, 3, shares.at[0], chan=partner)
         part_copy.start()
 
         spill(cnt_out, count)
@@ -400,11 +390,8 @@
         part_copy.wait_recv()
         mine = mc // 2
         pairs[mine] = part_s[...] + part_r[...]
-        pair_copies = []
         for j in range(1, npair):
-            copy = remote(pairs.at[mine], pairs.at[mine], sg.at[j], rg.at[j], chan=chan_peer[j])
-            copy.start()
-            pair_copies.append(copy)
+            remote(pairs.at[mine], pairs.at[mine], 4, shares.at[1], chan=chan_peer[j]).start()
 
         place = jnp.bitwise_xor(folded(dest), me) * lines + rank // LANES
         lane = rank & (LANES - 1)
@@ -412,18 +399,18 @@
         far_half = list(range(nrows - 1, half_rows - 1, -1))
         returns = [list(range(half_rows)), far_half]
         for slots in returns:
-            for d in slots:
-                if d > 0:
-                    back_copies[d].wait_recv()
+            first = max(1, min(slots))
+            wait_all(back_r.at[first : max(slots) + 1], back.at[first // half_rows])
             for d in slots:
                 for t in range(lines):
                     here = place == d * lines + t
                     for f in range(fields):
                         found[f] = jnp.where(here, take(back_r[d, f, t : t + 1], lane), found[f])
         for slots in returns:
-            for d, copy in scale_copies:
-                if d in slots:
-                    copy.wait_recv()
+            wait_all(
+                scale_r.at[nrows : nrows + (nchan - 1) * len(slots)],
+                scales.at[slots[0] // half_rows],
+            )
             for d in slots:
                 for t in range(lines):
                     here = place == d * lines + t
@@ -437,18 +424,17 @@
             turned[f * many : (f + 1) * many] = found[f] * scale
         for k in range(many):
             dep_out[:, k * LANES : (k + 1) * LANES] = turned[pl.ds(k, fields, stride=many), :]
-        for copy in pair_copies:
-            copy.wait_recv()
+        wait_all(pairs.at[1:], shares.at[1])
         spread = pairs[0]
         for p in range(1, npair):
             spread = spread + pairs[p]
         spill(spr_out, spread)
 
-        for copies in (out_copies, back_copies):
-            for copy in copies.values():
-                copy.wait_send()
-        for copy in [part_copy] + pair_copies + [copy for _, copy in scale_copies]:
-            copy.wait_send()
+        wait_all(sent.at[1:], send.at[0])
+        wait_all(back_s.at[1:], send.at[1])
+        wait_all(scale_r.at[nrows:], send.at[2])
+        part_copy.wait_send()
+        wait_all(pairs.at[1:], send.at[4])
 
     rows_summed = QS * 4 * fields + -(-QS // PACK) * PACK
     rows_looked = -(-(fields + 1) * QS // PACK) * PACK
@@ -512,16 +498,11 @@
             pltpu.VMEM((fields * obs // LANES, LANES), F32),
             pltpu.SemaphoreType.REGULAR,
             dma((4,)),
-            dma((nrows,)),
-            dma((nrows,)),
-            dma((1,)),
-            dma((1,)),
-            dma((npair,)),
-            dma((npair,)),
-            dma((nrows,)),
-            dma((nrows,)),
-            dma((nchan * nrows,)),
-            dma((nchan * nrows,)),
+            dma((5,)),
+            dma((2,)),
+            dma((2,)),
+            dma((2,)),
+            dma((2,)),
         ],
         compiler_params=pltpu.CompilerParams(
             collective_id=0, has_side_effects=True, vmem_limit_bytes=32 * 1024 * 1024

time: 18.7 us -> 17.9 us (0.957)
  Pallas kernels: 17.9 us -> 17 us
    pallas_call x1, Pallas kernels: 17.1 us -> 16.3 us  [body(): pl.pallas_call(functools.partial(kernel, nrows, nchan), out_shape=tuple((...]
where the time goes in v4:
time: 17.9 us; the launch traced here: 17.6 us
  Pallas kernels  17 us (95%)
  between operations  0.64 us (4%)
    pallas_call x1, Pallas kernels, body(): pl.pallas_call(functools.partial(kernel, nrows, nchan), out_shape=tuple((...  16.3 us
    pallas_call x1, Pallas kernels, body(): pl.pallas_call(finish, out_shape=tuple((jax.ShapeDtypeStruct(s, t) for s,...  0.74 us

profile of v4, /device:TPU:0, one launch (start us, length us, event | category | flops | bytes accessed | tf_op | source)
XLA Modules:
  0.0 17.6 jit_solution(8506245443403699234)
XLA Ops:
  0.6 16.3 %shard_map.83 = (s32[4,1440]{1,0:T(4,128)S(1)}, f32[4,4,1440]{2,1,0:T(4,128)S(1)}, f32[4,4,1440]{2,1,0:T(4,128)S(1)}, f32[4,1440]{1,0:T(4,128)S(1)}, f32[4,2048]{1,0:T(4,128)S(1)}) custom-call(f32[4,2048]{1,0:T(4,128)} %rad_in.1, s32[1,2048]{1,0:T(1,128)} %bitcast.3, s32[1,2048]{1,0:T(1,128)} %bitcast.4, s32[1,2048]{1,0:T(1,128)} %bitcast.5), custom_call_target="tpu_custom_call" | custom-call | tf_op jit(solution)/shard_map/pallas_call | solution.py:478
  16.9 0.7 %shard_map.84 = (s32[4,1440]{1,0:T(4,128)}, f32[4,4,1440]{2,1,0:T(4,128)}, f32[4,4,1440]{2,1,0:T(4,128)}, f32[4,1440]{1,0:T(4,128)}, f32[4,2048]{1,0:T(4,128)}) custom-call(s32[4,1440]{1,0:T(4,128)S(1)} %get-tuple-element.10.refs_0_, f32[4,4,1440]{2,1,0:T(4,128)S(1)} %get-tuple-element.11.refs_1_, f32[4,4,1440]{2,1,0:T(4,128)S(1)} %get-tuple-element.12.refs_2_, ...), custom_call_target="tpu_custom_call" | custom-call | tf_op jit(solution)/shard_map/pallas_call | solution.py:521

commit v5 on v4

--- a/solution.py
+++ b/solution.py
@@ -201,7 +201,7 @@
     lines = cap // LANES
     npair = nchan // 2
     half_rows = nrows // 2
-    far = list(range(nrows - 1, 0, -1))
+    far = sorted(range(1, nrows), key=lambda d: (d // half_rows, d % 2, d), reverse=True)
     row_peer = [flip(me, d) for d in range(nrows)]
     chan_peer = [lax.rem(mc + 2 * j, nchan) for j in range(npair)]
     partner = flip(mc, 1)
@@ -302,7 +302,7 @@
     pl.semaphore_wait(barrier, nrows + nchan - 2)
     for d in far:
         remote(
-            sent.at[d], arrived.at[d], 0, came.at[d // half_rows], rows=row_peer[d]
+            sent.at[d], arrived.at[d], 0, came.at[d // half_rows + (d + 1) // nrows], rows=row_peer[d]
         ).start()
     for e in range(1, nchan):
         pl.semaphore_signal(ready, inc=1, device_id={"chan": flip(mc, e)}, device_id_type=MESH)
@@ -310,10 +310,11 @@
 
     def cells_all(acc_0, acc_1, *looks):
         accs = (acc_0, acc_1)
-        groups = [[0], list(range(1, half_rows)), list(range(half_rows, nrows))]
+        groups = [[0], list(range(1, half_rows)), list(range(half_rows, nrows - 1)), [nrows - 1]]
         for slots in groups:
             if slots[0] > 0:
-                wait_all(arrived.at[slots[0] : slots[-1] + 1], came.at[slots[0] // half_rows])
+                at = slots[0] // half_rows + (slots[0] + 1) // nrows
+                wait_all(arrived.at[slots[0] : slots[-1] + 1], came.at[at])
             product(accs, tiles_of(arrived, col_hot, slots), True)
 
         total = pltpu.matmul_pop(accs[0]) + pltpu.matmul_pop(accs[1])
@@ -406,6 +407,16 @@
                     here = place == d * lines + t
                     for f in range(fields):
                         found[f] = jnp.where(here, take(back_r[d, f, t : t + 1], lane), found[f])
+        wait_all(pairs.at[1:], shares.at[1])
+        spread = pairs[0]
+        for p in range(1, npair):
+            spread = spread + pairs[p]
+        spill(spr_out, spread)
+        wait_all(sent.at[1:], send.at[0])
+        wait_all(back_s.at[1:], send.at[1])
+        wait_all(scale_r.at[nrows:], send.at[2])
+        part_copy.wait_send()
+        wait_all(pairs.at[1:], send.at[4])
         for slots in returns:
             wait_all(
                 scale_r.at[nrows : nrows + (nchan - 1) * len(slots)],
@@ -424,17 +435,6 @@
             turned[f * many : (f + 1) * many] = found[f] * scale
         for k in range(many):
             dep_out[:, k * LANES : (k + 1) * LANES] = turned[pl.ds(k, fields, stride=many), :]
-        wait_all(pairs.at[1:], shares.at[1])
-        spread = pairs[0]
-        for p in range(1, npair):
-            spread = spread + pairs[p]
-        spill(spr_out, spread)
-
-        wait_all(sent.at[1:], send.at[0])
-        wait_all(back_s.at[1:], send.at[1])
-        wait_all(scale_r.at[nrows:], send.at[2])
-        part_copy.wait_send()
-        wait_all(pairs.at[1:], send.at[4])
 
     rows_summed = QS * 4 * fields + -(-QS // PACK) * PACK
     rows_looked = -(-(fields + 1) * QS // PACK) * PACK
@@ -499,7 +499,7 @@
             pltpu.SemaphoreType.REGULAR,
             dma((4,)),
             dma((5,)),
-            dma((2,)),
+            dma((3,)),
             dma((2,)),
             dma((2,)),
             dma((2,)),

time: 17.9 us -> 17.6 us (0.983)
  Pallas kernels: 17 us -> 16.7 us
    pallas_call x1, Pallas kernels: 16.3 us -> 16 us  [body(): pl.pallas_call(functools.partial(kernel, nrows, nchan), out_shape=tuple((...]
where the time goes in v5:
time: 17.6 us; the launch traced here: 17.4 us
  Pallas kernels  16.7 us (95%)
  between operations  0.64 us (4%)
    pallas_call x1, Pallas kernels, body(): pl.pallas_call(functools.partial(kernel, nrows, nchan), out_shape=tuple((...  16 us
    pallas_call x1, Pallas kernels, body(): pl.pallas_call(finish, out_shape=tuple((jax.ShapeDtypeStruct(s, t) for s,...  0.74 us

profile of v5, /device:TPU:0, one launch (start us, length us, event | category | flops | bytes accessed | tf_op | source)
XLA Modules:
  0.0 17.4 jit_solution(7085575700976103318)
XLA Ops:
  0.6 16.0 %shard_map.83 = (s32[4,1440]{1,0:T(4,128)S(1)}, f32[4,4,1440]{2,1,0:T(4,128)S(1)}, f32[4,4,1440]{2,1,0:T(4,128)S(1)}, f32[4,1440]{1,0:T(4,128)S(1)}, f32[4,2048]{1,0:T(4,128)S(1)}) custom-call(f32[4,2048]{1,0:T(4,128)} %rad_in.1, s32[1,2048]{1,0:T(1,128)} %bitcast.3, s32[1,2048]{1,0:T(1,128)} %bitcast.4, s32[1,2048]{1,0:T(1,128)} %bitcast.5), custom_call_target="tpu_custom_call" | custom-call | tf_op jit(solution)/shard_map/pallas_call | solution.py:478
  16.6 0.7 %shard_map.84 = (s32[4,1440]{1,0:T(4,128)}, f32[4,4,1440]{2,1,0:T(4,128)}, f32[4,4,1440]{2,1,0:T(4,128)}, f32[4,1440]{1,0:T(4,128)}, f32[4,2048]{1,0:T(4,128)}) custom-call(s32[4,1440]{1,0:T(4,128)S(1)} %get-tuple-element.10.refs_0_, f32[4,4,1440]{2,1,0:T(4,128)S(1)} %get-tuple-element.11.refs_1_, f32[4,4,1440]{2,1,0:T(4,128)S(1)} %get-tuple-element.12.refs_2_, ...), custom_call_target="tpu_custom_call" | custom-call | tf_op jit(solution)/shard_map/pallas_call | solution.py:521

commit v6 on v5

--- a/solution.py
+++ b/solution.py
@@ -209,11 +209,11 @@
     def wait_all(ref, semaphore):
         pltpu.make_async_copy(ref, ref, semaphore).wait()
 
-    def remote(src, dst, kind, recv, **to):
+    def remote(src, dst, recv, **to):
         return pltpu.make_async_remote_copy(
             src_ref=src,
             dst_ref=dst,
-            send_sem=send.at[kind],
+            send_sem=send.at[0],
             recv_sem=recv,
             device_id=to,
             device_id_type=MESH,
@@ -227,7 +227,7 @@
     for e in range(1, nchan):
         pl.semaphore_signal(barrier, inc=1, device_id={"chan": flip(mc, e)}, device_id_type=MESH)
     fetches = [
-        pltpu.make_async_copy(a, b, ins.at[i])
+        pltpu.make_async_copy(a, b, ins.at[min(i, 1)])
         for i, (a, b) in enumerate(
             ((band_in, band_ref), (rad_in, rad_ref), (rib_in, rib_ref), (col_in, col_ref))
         )
@@ -249,8 +249,7 @@
             hots.append(low_hot(ranks[k] - upper * wide, LOW))
             names = jnp.bitwise_xor(dest[:, k * LANES : (k + 1) * LANES], me)
             keys.append(packed(names.astype(F32) * parts + upper))
-        for fetch in fetches[1:]:
-            fetch.wait()
+        wait_all(staged.at[: (fields + 2) * obs // LANES], ins.at[1])
         high, rest = two(rad_ref[...])
         middle, low = two(rest)
         col = col_ref[...]
@@ -302,7 +301,7 @@
     pl.semaphore_wait(barrier, nrows + nchan - 2)
     for d in far:
         remote(
-            sent.at[d], arrived.at[d], 0, came.at[d // half_rows + (d + 1) // nrows], rows=row_peer[d]
+            sent.at[d], arrived.at[d], came.at[d // half_rows + (d + 1) // nrows], rows=row_peer[d]
         ).start()
     for e in range(1, nchan):
         pl.semaphore_signal(ready, inc=1, device_id={"chan": flip(mc, e)}, device_id_type=MESH)
@@ -312,6 +311,9 @@
         accs = (acc_0, acc_1)
         groups = [[0], list(range(1, half_rows)), list(range(half_rows, nrows - 1)), [nrows - 1]]
         for slots in groups:
+            if slots[0] == nrows - 1:
+                wait_all(sent.at[1:], send.at[0])
+                pl.semaphore_wait(ready, nchan - 1)
             if slots[0] > 0:
                 at = slots[0] // half_rows + (slots[0] + 1) // nrows
                 wait_all(arrived.at[slots[0] : slots[-1] + 1], came.at[at])
@@ -345,7 +347,6 @@
             pltpu.matmul_acc_lhs(acc, table[0], load_staged_rhs=register)
             pltpu.matmul_acc_lhs(acc, table[1])
 
-        pl.semaphore_wait(ready, nchan - 1)
         for i in range(min(len(looks), len(tiles))):
             issue(i)
         for i, tile in enumerate(tiles):
@@ -371,17 +372,16 @@
                     remote(
                         target.at[d, fields],
                         scale_r.at[slot],
-                        2,
                         scales.at[d // half_rows],
                         rows=row_peer[d],
                         chan=flip(mc, e),
                     ).start()
                 if d > 0:
                     remote(
-                        back_s.at[d], back_r.at[d], 1, back.at[d // half_rows], rows=row_peer[d]
+                        back_s.at[d], back_r.at[d], back.at[d // half_rows], rows=row_peer[d]
                     ).start()
         part_s[...] = partial
-        part_copy = remote(part_s, part_r, 3, shares.at[0], chan=partner)
+        part_copy = remote(part_s, part_r, shares.at[0], chan=partner)
         part_copy.start()
 
         spill(cnt_out, count)
@@ -392,7 +392,7 @@
         mine = mc // 2
         pairs[mine] = part_s[...] + part_r[...]
         for j in range(1, npair):
-            remote(pairs.at[mine], pairs.at[mine], 4, shares.at[1], chan=chan_peer[j]).start()
+            remote(pairs.at[mine], pairs.at[mine], shares.at[1], chan=chan_peer[j]).start()
 
         place = jnp.bitwise_xor(folded(dest), me) * lines + rank // LANES
         lane = rank & (LANES - 1)
@@ -412,11 +412,8 @@
         for p in range(1, npair):
             spread = spread + pairs[p]
         spill(spr_out, spread)
-        wait_all(sent.at[1:], send.at[0])
-        wait_all(back_s.at[1:], send.at[1])
-        wait_all(scale_r.at[nrows:], send.at[2])
-        part_copy.wait_send()
-        wait_all(pairs.at[1:], send.at[4])
+        lent = (nrows - 1) * (fields + 1) + (nchan - 1) * nrows
+        wait_all(staged.at[: lent * lines + npair * QS * LOW // LANES], send.at[0])
         for slots in returns:
             wait_all(
                 scale_r.at[nrows : nrows + (nchan - 1) * len(slots)],
@@ -485,7 +482,7 @@
             pltpu.VMEM((1, obs), jnp.int32),
             pltpu.VMEM((1, obs), jnp.int32),
             pltpu.VMEM((1, obs), jnp.int32),
-            pltpu.VMEM((nrows * lines * 8, LANES), F32),
+            pltpu.VMEM((nrows * lines * 16, LANES), F32),
             pltpu.VMEM((nrows, fields + 1, lines, LANES), F32),
             pltpu.VMEM((nrows, fields + 1, lines, LANES), F32),
             pltpu.VMEM((nrows, LOW, cap), BF16),
@@ -497,8 +494,8 @@
             pltpu.VMEM((nchan * nrows, lines, LANES), F32),
             pltpu.VMEM((fields * obs // LANES, LANES), F32),
             pltpu.SemaphoreType.REGULAR,
-            dma((4,)),
-            dma((5,)),
+            dma((2,)),
+            dma((1,)),
             dma((3,)),
             dma((2,)),
             dma((2,)),

time: 17.6 us -> 17.5 us (level)
  no operation moved by 1% of the time
where the time goes in v6:
time: 17.5 us; the launch traced here: 17.2 us
  Pallas kernels  16.6 us (95%)
  between operations  0.64 us (4%)
    pallas_call x1, Pallas kernels, body(): pl.pallas_call(functools.partial(kernel, nrows, nchan), out_shape=tuple((...  15.9 us
    pallas_call x1, Pallas kernels, body(): pl.pallas_call(finish, out_shape=tuple((jax.ShapeDtypeStruct(s, t) for s,...  0.74 us

profile of v6, /device:TPU:0, one launch (start us, length us, event | category | flops | bytes accessed | tf_op | source)
XLA Modules:
  0.0 17.2 jit_solution(18397339615236426469)
XLA Ops:
  0.6 15.9 %shard_map.83 = (s32[4,1440]{1,0:T(4,128)S(1)}, f32[4,4,1440]{2,1,0:T(4,128)S(1)}, f32[4,4,1440]{2,1,0:T(4,128)S(1)}, f32[4,1440]{1,0:T(4,128)S(1)}, f32[4,2048]{1,0:T(4,128)S(1)}) custom-call(f32[4,2048]{1,0:T(4,128)} %rad_in.1, s32[1,2048]{1,0:T(1,128)} %bitcast.3, s32[1,2048]{1,0:T(1,128)} %bitcast.4, s32[1,2048]{1,0:T(1,128)} %bitcast.5), custom_call_target="tpu_custom_call" | custom-call | tf_op jit(solution)/shard_map/pallas_call | solution.py:475
  16.5 0.7 %shard_map.84 = (s32[4,1440]{1,0:T(4,128)}, f32[4,4,1440]{2,1,0:T(4,128)}, f32[4,4,1440]{2,1,0:T(4,128)}, f32[4,1440]{1,0:T(4,128)}, f32[4,2048]{1,0:T(4,128)}) custom-call(s32[4,1440]{1,0:T(4,128)S(1)} %get-tuple-element.10.refs_0_, f32[4,4,1440]{2,1,0:T(4,128)S(1)} %get-tuple-element.11.refs_1_, f32[4,4,1440]{2,1,0:T(4,128)S(1)} %get-tuple-element.12.refs_2_, ...), custom_call_target="tpu_custom_call" | custom-call | tf_op jit(solution)/shard_map/pallas_call | solution.py:518

commit v7 on v6

--- a/solution.py
+++ b/solution.py
@@ -186,6 +186,7 @@
     back_r,
     scale_r,
     turned,
+    ledger,
     ready,
     ins,
     send,
@@ -209,11 +210,11 @@
     def wait_all(ref, semaphore):
         pltpu.make_async_copy(ref, ref, semaphore).wait()
 
-    def remote(src, dst, recv, **to):
+    def remote(src, dst, recv, kind=0, **to):
         return pltpu.make_async_remote_copy(
             src_ref=src,
             dst_ref=dst,
-            send_sem=send.at[0],
+            send_sem=send.at[kind],
             recv_sem=recv,
             device_id=to,
             device_id_type=MESH,
@@ -381,7 +382,7 @@
                         back_s.at[d], back_r.at[d], back.at[d // half_rows], rows=row_peer[d]
                     ).start()
         part_s[...] = partial
-        part_copy = remote(part_s, part_r, shares.at[0], chan=partner)
+        part_copy = remote(part_s, part_r, shares.at[0], 1, chan=partner)
         part_copy.start()
 
         spill(cnt_out, count)
@@ -392,7 +393,7 @@
         mine = mc // 2
         pairs[mine] = part_s[...] + part_r[...]
         for j in range(1, npair):
-            remote(pairs.at[mine], pairs.at[mine], shares.at[1], chan=chan_peer[j]).start()
+            remote(pairs.at[mine], pairs.at[mine], shares.at[1], 1, chan=chan_peer[j]).start()
 
         place = jnp.bitwise_xor(folded(dest), me) * lines + rank // LANES
         lane = rank & (LANES - 1)
@@ -413,7 +414,8 @@
             spread = spread + pairs[p]
         spill(spr_out, spread)
         lent = (nrows - 1) * (fields + 1) + (nchan - 1) * nrows
-        wait_all(staged.at[: lent * lines + npair * QS * LOW // LANES], send.at[0])
+        wait_all(ledger.at[:lent], send.at[0])
+        wait_all(pairs, send.at[1])
         for slots in returns:
             wait_all(
                 scale_r.at[nrows : nrows + (nchan - 1) * len(slots)],
@@ -482,7 +484,7 @@
             pltpu.VMEM((1, obs), jnp.int32),
             pltpu.VMEM((1, obs), jnp.int32),
             pltpu.VMEM((1, obs), jnp.int32),
-            pltpu.VMEM((nrows * lines * 16, LANES), F32),
+            pltpu.VMEM((nrows * lines * 8, LANES), F32),
             pltpu.VMEM((nrows, fields + 1, lines, LANES), F32),
             pltpu.VMEM((nrows, fields + 1, lines, LANES), F32),
             pltpu.VMEM((nrows, LOW, cap), BF16),
@@ -493,9 +495,10 @@
             pltpu.VMEM((nrows, fields + 1, lines, LANES), F32),
             pltpu.VMEM((nchan * nrows, lines, LANES), F32),
             pltpu.VMEM((fields * obs // LANES, LANES), F32),
+            pltpu.VMEM((nrows * (fields + nchan), lines, LANES), F32),
             pltpu.SemaphoreType.REGULAR,
             dma((2,)),
-            dma((1,)),
+            dma((2,)),
             dma((3,)),
             dma((2,)),
             dma((2,)),

time: 17.5 us -> 17.5 us (level)
  no operation moved by 1% of the time
where the time goes in v7:
time: 17.5 us; the launch traced here: 17.2 us
  Pallas kernels  16.6 us (95%)
  between operations  0.64 us (4%)
    pallas_call x1, Pallas kernels, body(): pl.pallas_call(functools.partial(kernel, nrows, nchan), out_shape=tuple((...  15.9 us
    pallas_call x1, Pallas kernels, body(): pl.pallas_call(finish, out_shape=tuple((jax.ShapeDtypeStruct(s, t) for s,...  0.74 us

profile of v7, /device:TPU:0, one launch (start us, length us, event | category | flops | bytes accessed | tf_op | source)
XLA Modules:
  0.0 17.2 jit_solution(512432179701512707)
XLA Ops:
  0.6 15.9 %shard_map.83 = (s32[4,1440]{1,0:T(4,128)S(1)}, f32[4,4,1440]{2,1,0:T(4,128)S(1)}, f32[4,4,1440]{2,1,0:T(4,128)S(1)}, f32[4,1440]{1,0:T(4,128)S(1)}, f32[4,2048]{1,0:T(4,128)S(1)}) custom-call(f32[4,2048]{1,0:T(4,128)} %rad_in.1, s32[1,2048]{1,0:T(1,128)} %bitcast.3, s32[1,2048]{1,0:T(1,128)} %bitcast.4, s32[1,2048]{1,0:T(1,128)} %bitcast.5), custom_call_target="tpu_custom_call" | custom-call | tf_op jit(solution)/shard_map/pallas_call | solution.py:477
  16.5 0.7 %shard_map.84 = (s32[4,1440]{1,0:T(4,128)}, f32[4,4,1440]{2,1,0:T(4,128)}, f32[4,4,1440]{2,1,0:T(4,128)}, f32[4,1440]{1,0:T(4,128)}, f32[4,2048]{1,0:T(4,128)}) custom-call(s32[4,1440]{1,0:T(4,128)S(1)} %get-tuple-element.10.refs_0_, f32[4,4,1440]{2,1,0:T(4,128)S(1)} %get-tuple-element.11.refs_1_, f32[4,4,1440]{2,1,0:T(4,128)S(1)} %get-tuple-element.12.refs_2_, ...), custom_call_target="tpu_custom_call" | custom-call | tf_op jit(solution)/shard_map/pallas_call | solution.py:521

commit v8 on v7

--- a/solution.py
+++ b/solution.py
@@ -445,16 +445,19 @@
 
 
 def finish(*refs):
-    half = (len(refs) - 1) // 2
-    sems = refs[-1]
-    copies = [
-        pltpu.make_async_copy(a, b, sems.at[i])
-        for i, (a, b) in enumerate(zip(refs[:half], refs[half : 2 * half]))
-    ]
-    for copy in copies:
-        copy.start()
-    for copy in copies:
-        copy.wait()
+    half = len(refs) // 2
+
+    def store(sems):
+        copies = [
+            pltpu.make_async_copy(a, b, sems.at[i])
+            for i, (a, b) in enumerate(zip(refs[:half], refs[half:]))
+        ]
+        for copy in copies:
+            copy.start()
+        for copy in copies:
+            copy.wait()
+
+    pl.run_scoped(store, pltpu.SemaphoreType.DMA((half,)))
 
 
 def body(radiances, band, row_in_band, column):
@@ -523,7 +526,6 @@
         out_shape=tuple(jax.ShapeDtypeStruct(s, t) for s, t in shapes),
         in_specs=[vmem] * len(shapes),
         out_specs=(anywhere,) * len(shapes),
-        scratch_shapes=[dma((len(shapes),))],
         compiler_params=pltpu.CompilerParams(vmem_limit_bytes=32 * 1024 * 1024),
     )(*held)
 

time: 17.5 us -> 17.4 us (level)
  no operation moved by 1% of the time
where the time goes in v8:
time: 17.4 us; the launch traced here: 17.2 us
  Pallas kernels  16.6 us (95%)
  between operations  0.64 us (4%)
    pallas_call x1, Pallas kernels, body(): pl.pallas_call(functools.partial(kernel, nrows, nchan), out_shape=tuple((...  15.9 us
    pallas_call x1, Pallas kernels, body(): pl.pallas_call(finish, out_shape=tuple((jax.ShapeDtypeStruct(s, t) for s,...  0.7 us

profile of v8, /device:TPU:0, one launch (start us, length us, event | category | flops | bytes accessed | tf_op | source)
XLA Modules:
  0.0 17.2 jit_solution(1216881273578606397)
XLA Ops:
  0.6 15.9 %shard_map.83 = (s32[4,1440]{1,0:T(4,128)S(1)}, f32[4,4,1440]{2,1,0:T(4,128)S(1)}, f32[4,4,1440]{2,1,0:T(4,128)S(1)}, f32[4,1440]{1,0:T(4,128)S(1)}, f32[4,2048]{1,0:T(4,128)S(1)}) custom-call(f32[4,2048]{1,0:T(4,128)} %rad_in.1, s32[1,2048]{1,0:T(1,128)} %bitcast.3, s32[1,2048]{1,0:T(1,128)} %bitcast.4, s32[1,2048]{1,0:T(1,128)} %bitcast.5), custom_call_target="tpu_custom_call" | custom-call | tf_op jit(solution)/shard_map/pallas_call | solution.py:480
  16.5 0.7 %shard_map.84 = (s32[4,1440]{1,0:T(4,128)}, f32[4,4,1440]{2,1,0:T(4,128)}, f32[4,4,1440]{2,1,0:T(4,128)}, f32[4,1440]{1,0:T(4,128)}, f32[4,2048]{1,0:T(4,128)}) custom-call(s32[4,1440]{1,0:T(4,128)S(1)} %get-tuple-element.10.refs_0_, f32[4,4,1440]{2,1,0:T(4,128)S(1)} %get-tuple-element.11.refs_1_, f32[4,4,1440]{2,1,0:T(4,128)S(1)} %get-tuple-element.12.refs_2_, ...), custom_call_target="tpu_custom_call" | custom-call | tf_op jit(solution)/shard_map/pallas_call | solution.py:524
